TPU v7x, 32 devices: a whole 2x2x4 slice. The times are simulated.
32 devices in a mesh: feat: 8 (over z, y), samp: 4 (over x, core).
Axes of the slice: x: 2, y: 2, z: 4, core: 2. Of those that a mesh axis runs over, the one named last changes fastest.
Arguments:
- design: bfloat16 [14336, 8192], P('samp', 'feat'), may hold values from -0.0625 to 0.0625
- targets: bfloat16 [14336, 128], P('samp'), may hold values from -26 to 26
- warm_start: float32 [8192, 128], P('feat'), may hold values from -0.6 to 0.6
- active_mask: int32 [2, 8192], P(None, 'feat'), may hold values 0 or 1
- penalty_index: int32 [1], replicated, may hold values from 0 to 7
Outputs:
- coefficients: float32 [8192, 128], P('feat')
- correlations: float32 [3, 8192], P(None, 'feat')
- relative_gaps: float32 [3], replicated
- pruned_counts: float32 [2], replicated
All inputs are finite; a program needn't handle non-finite values. No bound on the sum of `active_mask` on one device may be relied on, other than what follows from the above.
Results may differ from a plain program's by a relative error of at most 0.0024.
The roundings to bfloat16 on the way count: a program that leaves them out, or rounds other values in their place, can miss the bound.
Values may be sent and summed in bfloat16 or wider, within the bound.
A program may use at most 64 MiB of HBM per device.

v0:
```python
import functools

import jax
import jax.numpy as jnp
from jax import lax
from jax.experimental import pallas as pl
from jax.experimental.pallas import tpu as pltpu
from jax.sharding import PartitionSpec as P

ITERS = 2
F32 = jnp.float32
BF16 = jnp.bfloat16
LANES = 128
SHARE = BF16
GRAD = BF16
H = 2
STATS = 16


def fold(row, combine):
    pieces = [row[:, at : at + LANES] for at in range(0, row.shape[1], LANES)]
    return functools.reduce(combine, pieces)


def top(matrix):
    return jnp.max(jnp.max(matrix, axis=0, keepdims=True), axis=1, keepdims=True)


def total_of(matrix):
    return jnp.sum(jnp.sum(matrix, axis=0, keepdims=True), axis=1, keepdims=True)


def column_norms(matrix):
    return jnp.sqrt(jnp.sum(matrix * matrix, axis=0, keepdims=True))


def kernel(
    sizes, stored, targets, warm, mask, index, coef_out, corr_out, info_out,
    design, gacc, mine, ysend, yrecv, zsend, zrecv, resid, turned, gsend, grecv, half, cur, squares,
    sqrecv, coefs, norms, exf, exs,
    y_s, y_r, z_s, z_r, a_s, a_r, b_s, b_r, g_s, g_r, h_s, h_r, q_s, q_r, c_s, c_r, n_s, n_r,
    ef_s, ef_r, es_s, es_r, d_s,
):
    F, Z, S = sizes
    R, C = design.shape
    K = targets.shape[1]
    B = R // F
    W = C // S
    b = B // H
    f = lax.axis_index("feat")
    s = lax.axis_index("samp")
    z, y = f // 2, lax.rem(f, 2)
    partner = z * 2 + 1 - y

    def ahead_z(off):
        return lax.rem(z + off, Z)

    def behind_z(off):
        return lax.rem(z - off + Z, Z)

    def ahead_s(off):
        return lax.rem(s + off, S)

    def feat_copy(src, dst, send, recv, to):
        return pltpu.make_async_remote_copy(
            src_ref=src, dst_ref=dst, send_sem=send, recv_sem=recv,
            device_id={"feat": to}, device_id_type=pl.DeviceIdType.MESH,
        )

    def samp_copy(src, dst, send, recv, off):
        return pltpu.make_async_remote_copy(
            src_ref=src, dst_ref=dst, send_sem=send, recv_sem=recv,
            device_id={"samp": ahead_s(off)}, device_id_type=pl.DeviceIdType.MESH,
        )

    def rows_of(slot):
        return pl.ds(pl.multiple_of(slot * B, B), B)

    def half_of(slot, h):
        return pl.ds(pl.multiple_of(slot * B + h * b, b), b)

    def copy_d(own, off):
        at = rows_of(ahead_z(off) * 2 + (y if own else 1 - y))
        return pltpu.make_async_copy(stored.at[at, :], design.at[at, :], d_s.at[own, off])

    def copy_y(t, off, h):
        at = (t, off, h)
        return feat_copy(ysend.at[at], yrecv.at[at], y_s.at[at], y_r.at[at], partner)

    def copy_z(t, off, h):
        at = (t, off, h)
        return feat_copy(zsend.at[at], zrecv.at[at], z_s.at[at], z_r.at[at], ahead_z(off) * 2 + y)

    def copy_a(t, off, h):
        at = (t, off, h)
        own = resid.at[t, f, h]
        return feat_copy(own, own, a_s.at[at], a_r.at[at], ahead_z(off) * 2 + y)

    def copy_b(t, off, h):
        at = (t, off, h)
        block = resid.at[t, behind_z(off) * 2 + y, h]
        return feat_copy(block, block, b_s.at[at], b_r.at[at], partner)

    def copy_g(t, off):
        return samp_copy(gsend.at[t, off], grecv.at[t, off], g_s.at[t, off], g_r.at[t, off], off)

    def copy_h(t, off):
        return samp_copy(half.at[t, s], half.at[t, s], h_s.at[t, off], h_r.at[t, off], off)

    def copy_q(off):
        return samp_copy(squares.at[ahead_s(off)], sqrecv.at[off], q_s.at[off], q_r.at[off], off)

    def copy_c(off):
        return samp_copy(coefs.at[s], coefs.at[s], c_s.at[off], c_r.at[off], off)

    def copy_n(off):
        return samp_copy(norms.at[s], norms.at[s], n_s.at[off], n_r.at[off], off)

    def copy_ef(e, off):
        return feat_copy(
            exf.at[e, f], exf.at[e, f], ef_s.at[e, off], ef_r.at[e, off], lax.rem(f + off, F)
        )

    def copy_es(e, off):
        return samp_copy(exs.at[e, s], exs.at[e, s], es_s.at[e, off], es_r.at[e, off], off)

    def each(count, body, first=0):
        def step(at, carry):
            body(at)
            return carry

        lax.fori_loop(first, count, step, 0)

    for own in range(2):
        for i in range(Z):
            copy_d(own, (i + 1) % Z).start()
    barrier = pltpu.get_barrier_semaphore()
    for off in range(1, F):
        pl.semaphore_signal(
            barrier, inc=1, device_id={"feat": lax.rem(f + off, F)}, device_id_type=pl.DeviceIdType.MESH
        )
    for off in range(1, S):
        pl.semaphore_signal(
            barrier, inc=1, device_id={"samp": ahead_s(off)}, device_id_type=pl.DeviceIdType.MESH
        )

    half[0] = warm[...].astype(BF16).reshape(S, W, K)
    norms[s] = jnp.zeros((8, W), F32)
    cur[...] = warm[pl.ds(pl.multiple_of(s * W, W), W), :].T
    pl.semaphore_wait(barrier, F - 1 + S - 1)

    def share(t, slot, h):
        block = design[half_of(slot, h), :]
        return jnp.dot(block, half[t].reshape(C, K), preferred_element_type=F32)

    def grad_chunk(t, k, chunk, first, last):
        turned[...] = chunk.T
        rows = pl.ds(pl.multiple_of(k * 2 * B, 2 * B), 2 * B)

        def part(off):
            at = pl.ds(pl.multiple_of(ahead_s(off) * W, W), W)
            piece = jnp.dot(turned[...], design[rows, at], preferred_element_type=F32)
            return piece if first else gacc[off] + piece

        def step(off):
            if last:
                gsend[t, off] = part(off).astype(GRAD)
                copy_g(t, off).start()
            else:
                gacc[off] = part(off)

        each(S, step, 1)
        gacc[0] = part(0)

    def grad_sum(t, own):
        for off in range(1, S):
            copy_g(t, off).wait_recv()
            own = own + grecv[t, off].astype(F32)
        return own

    def square_columns():
        tall = 16

        def body(at, acc):
            rows = design[pl.ds(pl.multiple_of(at * tall, tall), tall), :].astype(F32)
            rows = rows * rows
            return acc + rows[:8] + rows[8:]

        acc = lax.fori_loop(0, R // tall, body, jnp.zeros((8, C), F32), unroll=4)
        for c in range(S):
            squares[c] = acc[:, c * W : (c + 1) * W]
        for off in range(1, S):
            copy_q(off).start()

    sums = []
    bn_rows, gmax_rows, pruned_rows = [], [], []
    penalty = None
    step_sizes = None
    for t in range(ITERS + 1):

        for h in range(H):

            def send_y(i):
                off = lax.rem(i + 1, Z)
                if t == 0 and h == 0:
                    copy_d(0, off).wait()
                ysend[t, off, h] = share(t, ahead_z(off) * 2 + 1 - y, h).astype(SHARE)
                copy_y(t, off, h).start()

            each(Z, send_y)

        for h in range(H):

            def send_z(off):
                if t == 0 and h == 0:
                    copy_d(1, off).wait()
                mine[...] = share(t, ahead_z(off) * 2 + y, h)
                copy_y(t, off, h).wait_recv()
                zsend[t, off, h] = (mine[...] + yrecv[t, off, h].astype(F32)).astype(SHARE)
                copy_z(t, off, h).start()

            each(Z, send_z, 1)
        if t == 0:
            copy_d(1, 0).wait()
            for k in range(Z):
                chunk = targets[k * 2 * B : (k + 1) * 2 * B, :]
                grad_chunk(ITERS + 1, k, chunk, k == 0, k == Z - 1)
            corr_own = gacc[0]
            square_columns()
            corr = grad_sum(ITERS + 1, corr_own)
            exf[0, f] = jnp.broadcast_to(fold(column_norms(corr), jnp.maximum), (STATS, LANES))
            for off in range(1, F):
                copy_ef(0, off).start()
        bn_rows.append(fold(column_norms(cur[...]), jnp.add))
        rr = jnp.zeros((1, K), F32)
        ry = jnp.zeros((1, K), F32)
        for h in range(H):
            fitted = share(t, f, h)
            copy_y(t, 0, h).wait_recv()
            fitted = fitted + yrecv[t, 0, h].astype(F32)
            for off in range(1, Z):
                copy_z(t, off, h).wait_recv()
                fitted = fitted + zrecv[t, off, h].astype(F32)
            own_targets = targets[half_of(f, h), :].astype(F32)
            rounded = (own_targets - fitted).astype(BF16)
            resid[t, f, h] = rounded
            for off in range(1, Z):
                copy_a(t, off, h).start()
            copy_b(t, 0, h).start()
            wide = rounded.astype(F32)
            rr = rr + jnp.sum(wide * wide, axis=0, keepdims=True)
            ry = ry + jnp.sum(wide * own_targets, axis=0, keepdims=True)
        sums.append((rr, ry))
        for off in range(Z):
            if off + 1 < Z:
                for h in range(H):
                    copy_a(t, off + 1, h).wait_recv()
                    copy_b(t, off + 1, h).start()
            if t == 0 and off == Z - 2:
                for at in range(1, F):
                    copy_ef(0, at).wait_recv()
                exs[0, s] = functools.reduce(jnp.maximum, [exf[0, at] for at in range(F)])
                for at in range(1, S):
                    copy_es(0, at).start()
            for h in range(H):
                copy_b(t, off, h).wait_recv()
            k = behind_z(off)
            chunk = resid[t, pl.ds(2 * k, 2)].reshape(2 * B, K)
            grad_chunk(t, k, chunk, off == 0, off == Z - 1)
        gradient = grad_sum(t, gacc[0])
        if t == 0:
            for off in range(1, S):
                copy_es(0, off).wait_recv()
            penalty_max = top(functools.reduce(jnp.maximum, [exs[0, at] for at in range(S)]))
            square = squares[s]
            for off in range(1, S):
                copy_q(off).wait_recv()
                square = square + sqrecv[off]
            step_sizes = 0.5 / (1.0 + jnp.sum(square, axis=0, keepdims=True))
            penalty = penalty_max / (8.0 + 4.0 * index[0].astype(F32))
        if t < ITERS:
            keep = mask[t : t + 1, pl.ds(pl.multiple_of(s * W, W), W)].astype(F32)
            moved = cur[...] + step_sizes * gradient
            moved_norms = column_norms(moved)
            cutoff = step_sizes * penalty
            factor = jnp.maximum(moved_norms - cutoff, 0.0) / jnp.maximum(moved_norms, cutoff)
            after = (keep * factor) * moved
            cur[...] = after
            upright = after.T
            half[t + 1, s] = upright.astype(BF16)
            for off in range(1, S):
                copy_h(t + 1, off).start()
            if t + 1 == ITERS:
                coefs[s] = upright
                for off in range(1, S):
                    copy_c(off).start()
            pruned_rows.append(fold(1.0 - keep, jnp.add))
        grad_norms = column_norms(gradient)
        norms[s, t : t + 1, :] = grad_norms
        gmax_rows.append(fold(grad_norms, jnp.maximum))
        if t < ITERS:
            for off in range(1, S):
                copy_h(t + 1, off).wait_recv()

    for off in range(1, S):
        copy_n(off).start()
    added = [row[0] for row in sums] + [row[1] for row in sums] + bn_rows + pruned_rows
    n_add = len(added)
    blank = jnp.zeros((STATS - n_add - len(gmax_rows), LANES), F32)
    exf[1, f] = jnp.concatenate(added + gmax_rows + [blank], axis=0)
    for off in range(1, F):
        copy_ef(1, off).start()

    def merge(tiles):
        plus = functools.reduce(jnp.add, tiles)
        most = functools.reduce(jnp.maximum, tiles)
        at = lax.broadcasted_iota(jnp.int32, plus.shape, 0)
        return jnp.where(at < n_add, plus, most)

    for off in range(1, F):
        copy_ef(1, off).wait_recv()
    exs[1, s] = merge([exf[1, at] for at in range(F)])
    for off in range(1, S):
        copy_es(1, off).start()
    for off in range(1, S):
        copy_c(off).wait_recv()
    coef_out[...] = coefs[...].reshape(C, K)
    for off in range(1, S):
        copy_n(off).wait_recv()
    for off in range(1, S):
        copy_es(1, off).wait_recv()
    merged = merge([exs[1, at] for at in range(S)])
    added_up = jnp.sum(merged, axis=1, keepdims=True)
    highest = jnp.max(merged, axis=1, keepdims=True)
    T = ITERS + 1
    lines = []
    for t in range(T):
        rr, ry, bn = (added_up[at : at + 1] for at in (t, T + t, 2 * T + t))
        scale = jnp.maximum(penalty, highest[n_add + t : n_add + t + 1])
        primal = 0.5 * rr + penalty * bn
        ratio = penalty / scale
        dual = ratio * ry - 0.5 * ratio * ratio * rr
        lines.append((primal - dual) / (primal + 1.0))
        for c in range(S):
            corr_out[t : t + 1, c * W : (c + 1) * W] = norms[c, t : t + 1, :] / scale
    for t in range(ITERS):
        lines.append(added_up[3 * T + t : 3 * T + t + 1])
    for at, line in enumerate(lines):
        info_out[at : at + 1, :] = jnp.broadcast_to(line, (1, LANES))

    for t in range(ITERS + 1):
        for h in range(H):

            def drain(off):
                copy_y(t, off, h).wait_send()
                copy_b(t, off, h).wait_send()

            def drain_line(off):
                copy_z(t, off, h).wait_send()
                copy_a(t, off, h).wait_send()

            each(Z, drain)
            each(Z, drain_line, 1)
    for off in range(1, S):
        for t in range(ITERS + 2):
            copy_g(t, off).wait_send()
        for t in range(1, ITERS + 1):
            copy_h(t, off).wait_send()
        copy_q(off).wait_send()
        copy_c(off).wait_send()
        copy_n(off).wait_send()
        copy_es(0, off).wait_send()
        copy_es(1, off).wait_send()
    for off in range(1, F):
        copy_ef(0, off).wait_send()
        copy_ef(1, off).wait_send()


def finish(coef, corr, info, coef_out, corr_out, gaps_out, pruned_out):
    coef_out[...] = coef[...]
    corr_out[...] = corr[...]
    for at in range(ITERS + 1):
        gaps_out[at] = info[at, 0]
    for at in range(ITERS):
        pruned_out[at] = info[ITERS + 1 + at, 0]


def fused(design, targets, warm_start, active_mask, penalty_index):
    F, S = lax.axis_size("feat"), lax.axis_size("samp")
    R, C = design.shape
    K = targets.shape[1]
    Z, B, W, T = F // 2, R // F, C // S, ITERS + 1
    dma = pltpu.SemaphoreType.DMA
    vmem = pl.BlockSpec(memory_space=pltpu.VMEM)
    coefficients, correlations, info = pl.pallas_call(
        functools.partial(kernel, (F, Z, S)),
        out_shape=(
            jax.ShapeDtypeStruct((C, K), F32),
            jax.ShapeDtypeStruct((T, C), F32),
            jax.ShapeDtypeStruct((8, LANES), F32),
        ),
        in_specs=[pl.BlockSpec(memory_space=pl.ANY)] + [vmem] * 3 + [pl.BlockSpec(memory_space=pltpu.SMEM)],
        out_specs=(vmem,) * 3,
        scratch_shapes=[
            pltpu.VMEM((R, C), BF16),
            pltpu.VMEM((S, K, W), F32),
            pltpu.VMEM((B // H, K), F32),
            pltpu.VMEM((T, Z, H, B // H, K), SHARE),
            pltpu.VMEM((T, Z, H, B // H, K), SHARE),
            pltpu.VMEM((T, Z, H, B // H, K), SHARE),
            pltpu.VMEM((T, Z, H, B // H, K), SHARE),
            pltpu.VMEM((T, F, H, B // H, K), BF16),
            pltpu.VMEM((K, 2 * B), BF16),
            pltpu.VMEM((T + 1, S, K, W), GRAD),
            pltpu.VMEM((T + 1, S, K, W), GRAD),
            pltpu.VMEM((T, S, W, K), BF16),
            pltpu.VMEM((K, W), F32),
            pltpu.VMEM((S, 8, W), F32),
            pltpu.VMEM((S, 8, W), F32),
            pltpu.VMEM((S, W, K), F32),
            pltpu.VMEM((S, 8, W), F32),
            pltpu.VMEM((2, F, STATS, LANES), F32),
            pltpu.VMEM((2, S, STATS, LANES), F32),
        ]
        + [dma((T, Z, H))] * 8
        + [dma((T + 1, S))] * 2
        + [dma((T, S))] * 2
        + [dma((S,))] * 6
        + [dma((2, F))] * 2
        + [dma((2, S))] * 2
        + [dma((2, Z))],
        compiler_params=pltpu.CompilerParams(
            collective_id=0, has_side_effects=True, vmem_limit_bytes=62 * 1024 * 1024
        ),
    )(design, targets, warm_start, active_mask, penalty_index)
    smem = pl.BlockSpec(memory_space=pltpu.SMEM)
    return pl.pallas_call(
        finish,
        out_shape=(
            jax.ShapeDtypeStruct((C, K), F32),
            jax.ShapeDtypeStruct((T, C), F32),
            jax.ShapeDtypeStruct((T,), F32),
            jax.ShapeDtypeStruct((ITERS,), F32),
        ),
        in_specs=[vmem, vmem, smem],
        out_specs=(vmem, vmem, smem, smem),
    )(coefficients, correlations, info)


def group_norms(matrix):
    return jnp.sqrt(jnp.sum(matrix * matrix, axis=1))


def transpose_product(design, right_side):
    return lax.dot_general(
        design, right_side, (((0,), (0,)), ((), ())), preferred_element_type=jnp.float32
    )


def plain(design, targets, warm_start, active_mask, penalty_index):
    row_count, col_count = design.shape
    feat_size = lax.axis_size("feat")
    feat_slot = lax.axis_index("feat")
    block_rows = row_count // feat_size
    samp_first = (lax.axis_index("samp") == 0).astype(jnp.float32)
    corr_local = transpose_product(design, targets)
    squares_local = jnp.sum(jnp.square(design.astype(jnp.float32)), axis=0)
    corr_y, column_squares = lax.psum((corr_local, squares_local), "samp")
    penalty_max = lax.pmax(jnp.max(group_norms(corr_y)), "feat")
    penalty = penalty_max / (8.0 + 4.0 * penalty_index[0].astype(jnp.float32))
    step_sizes = 0.5 / (1.0 + column_squares)
    current = warm_start
    correlations = []
    relative_gaps = []
    pruned_counts = []
    own_targets = lax.dynamic_slice_in_dim(targets, feat_slot * block_rows, block_rows, 0)
    for iteration in range(ITERS + 1):
        current_half = current.astype(jnp.bfloat16)
        fitted_part = jnp.dot(design, current_half, preferred_element_type=jnp.float32)
        fitted = lax.psum(fitted_part, "feat")
        residual_all = (targets.astype(jnp.float32) - fitted).astype(jnp.bfloat16)
        residual = lax.dynamic_slice_in_dim(residual_all, feat_slot * block_rows, block_rows, 0)
        grad_local = transpose_product(design, residual_all)
        resid_float = residual.astype(jnp.float32)
        rr_local = jnp.sum(resid_float * resid_float)
        ry_local = jnp.sum(resid_float * own_targets.astype(jnp.float32))
        bn_local = samp_first * jnp.sum(group_norms(current))
        if iteration < ITERS:
            keep = active_mask[iteration].astype(jnp.float32)
            pruned_local = samp_first * jnp.sum(1.0 - keep)
        else:
            pruned_local = jnp.zeros((), jnp.float32)
        gradient = lax.psum(grad_local, "samp")
        grad_norms = group_norms(gradient)
        local_max = jnp.max(grad_norms)
        grad_top = lax.pmax(local_max, "feat")
        rr_sum, ry_sum, bn_sum, pruned_sum = lax.psum(
            (rr_local, ry_local, bn_local, pruned_local), ("feat", "samp")
        )
        scale = jnp.maximum(penalty, grad_top)
        correlations.append(grad_norms / scale)
        primal = 0.5 * rr_sum + penalty * bn_sum
        ratio = penalty / scale
        dual = ratio * ry_sum - 0.5 * ratio * ratio * rr_sum
        relative_gaps.append((primal - dual) / (primal + 1.0))
        if iteration < ITERS:
            pruned_counts.append(pruned_sum)
            moved = current + step_sizes[:, None] * gradient
            moved_norms = group_norms(moved)
            cutoff = step_sizes * penalty
            factor = jnp.maximum(moved_norms - cutoff, 0.0) / jnp.maximum(moved_norms, cutoff)
            current = (keep * factor)[:, None] * moved
    return (current, jnp.stack(correlations), jnp.stack(relative_gaps), jnp.stack(pruned_counts))


def local(design, targets, warm_start, active_mask, penalty_index):
    feat, samp = lax.axis_size("feat"), lax.axis_size("samp")
    rows, cols = design.shape
    fits = (
        feat % 2 == 0
        and rows % (feat * 16 * H) == 0
        and (2 * rows // feat) % LANES == 0
        and cols % (samp * LANES) == 0
        and targets.shape[1] == LANES
    )
    form = fused if fits else plain
    return form(design, targets, warm_start, active_mask, penalty_index)


def solution(mesh):
    placed = (P("samp", "feat"), P("samp", None), P("feat", None), P(None, "feat"), P())
    return jax.shard_map(
        local,
        mesh=mesh,
        in_specs=placed,
        out_specs=(P("feat", None), P(None, "feat"), P(), P()),
        check_vma=False,
    )
```

profile of v0, /device:TPU:0, one launch (start us, length us, event | category | flops | bytes accessed | tf_op | source)
XLA Modules:
  0.0 143.5 jit_solution(14297619387682584560)
XLA Ops:
  1.3 140.3 %shard_map.84 = (f32[1024,128]{1,0:T(8,128)}, f32[3,1024]{1,0:T(4,128)}, f32[8,128]{1,0:T(8,128)}) custom-call(bf16[3584,1024]{1,0:T(8,128)(2,1)} %stored.1, bf16[3584,128]{1,0:T(8,128)(2,1)} %targets.1, f32[1024,128]{1,0:T(8,128)} %warm.1, s32[2,1024]{1,0:T(2,128)} %mask.1, s32[1]{0:T(128)S(6)} %copy.9.index), custom_call_target="tpu_custom_call" | custom-call | tf_op jit(solution)/shard_map/pallas_call | solution.py:395
  141.6 1.9 %shard_map.85 = (f32[1024,128]{1,0:T(8,128)}, f32[3,1024]{1,0:T(4,128)}, f32[3]{0:T(128)}, f32[2]{0:T(128)}) custom-call(f32[1024,128]{1,0:T(8,128)} %get-tuple-element.7.coef, f32[3,1024]{1,0:T(4,128)} %get-tuple-element.8.corr, f32[8,128]{1,0:T(8,128)} %get-tuple-element.9.info), custom_call_target="tpu_custom_call" | custom-call | tf_op jit(solution)/shard_map/pallas_call | solution.py:437
where the time goes:
time: 144 us; the launch traced here: 143 us
  Pallas kernels  142 us (99%)
    pallas_call x1, Pallas kernels, fused(): pl.pallas_call(functools.partial(kernel, (F, Z, S)), out_shape=(jax.Shape...  140 us

commit v1 on v0

v1 whole, which is shorter than its diff:
```python
import functools

import jax
import jax.numpy as jnp
from jax import lax
from jax.experimental import pallas as pl
from jax.experimental.pallas import tpu as pltpu
from jax.sharding import PartitionSpec as P

ITERS = 2
F32 = jnp.float32
BF16 = jnp.bfloat16
LANES = 128
GROUP = 256
PER = 2
LINE = 4
CORES = 2
STATS = 16
MESH = pl.DeviceIdType.MESH


def fold(row, combine):
    pieces = [row[:, at : at + LANES] for at in range(0, row.shape[1], LANES)]
    return functools.reduce(combine, pieces)


def column_norms(matrix):
    return jnp.sqrt(jnp.sum(matrix * matrix, axis=0, keepdims=True))


def kernel(
    stored, stored_targets, stored_warm, mask, index, coef_out, corr_out, info_out,
    design, targets, warm, half, cur, ysend, yrecv, zsend, frecv, erecv, resid, mine, turned,
    gacc, cacc, drecv, dcrecv, gsend, grecv, sqs, sqr, coefs, nrm, mx, sums, exf, exs,
    l_s, t_s, w_s, y_s, y_r, z_s, f_r, e_r, b_s, a_s, a_r, d_s, d_r, x_s, x_r, h_s, h_r, q_s, q_r,
    c_s, c_r, n_s, n_r, m_s, m_r, ef_s, ef_r, es_s, es_r,
):
    T = ITERS + 1
    F = exf.shape[0]
    S = exs.shape[0]
    R, C = design.shape
    K = targets.shape[1]
    H = R // 2
    G = H // GROUP
    b = GROUP // PER
    pieces = CORES * 2
    W = C // pieces
    f = lax.axis_index("feat")
    s = lax.axis_index("samp")
    z, y = f // 2, lax.rem(f, 2)
    x, c = s // CORES, lax.rem(s, CORES)
    mid = lax.rem((z + 1) // 2, 2)
    is_mid = mid == 1
    is_end = mid == 0
    me = f * CORES + c
    near = z + 1 - 2 * lax.rem(z, 2)
    across = {"feat": z * 2 + 1 - y}
    nearby = {"feat": near * 2 + y}
    middle = {"feat": (LINE - 1 - z) * 2 + y}
    sibling = {"samp": x * CORES + 1 - c}
    facing = {"samp": (1 - x) * CORES + c}

    def remote(src, dst, send, recv, to):
        return pltpu.make_async_remote_copy(
            src_ref=src, dst_ref=dst, send_sem=send, recv_sem=recv, device_id=to, device_id_type=MESH
        )

    def peer(off):
        to = lax.rem(me + off, F * CORES)
        return {"feat": to // CORES, "samp": x * CORES + lax.rem(to, CORES)}

    def rows_at(side, g):
        return pl.ds(pl.multiple_of(side * H + g * GROUP, GROUP), GROUP)

    def load(side, g):
        at = rows_at(side, g)
        return pltpu.make_async_copy(stored.at[at, :], design.at[at, :], l_s.at[side, g])

    load_targets = pltpu.make_async_copy(stored_targets, targets, t_s)
    load_warm = pltpu.make_async_copy(stored_warm, warm, w_s)

    def copy_y(t, k):
        at = (t, k)
        return remote(ysend.at[at], yrecv.at[at], y_s.at[at], y_r.at[at], across)

    def copy_fold(t, k):
        at = (t, k)
        return remote(zsend.at[at], frecv.at[at], z_s.at[at], f_r.at[at], nearby)

    def copy_middle(t, k):
        at = (t, k)
        return remote(zsend.at[at], erecv.at[at], z_s.at[at], e_r.at[at], middle)

    def copy_out(t, k):
        ref = resid.at[t, y, k]
        return remote(ref, ref, b_s.at[t, k], f_r.at[t, k], nearby)

    def copy_a(t, k):
        ref = resid.at[t, y, k]
        return remote(ref, ref, a_s.at[t, k], a_r.at[t, k], across)

    def copy_d(t, j):
        at = (t, j)
        if t == T:
            return remote(cacc.at[(1 - c) * 2 + j], dcrecv.at[j], d_s.at[at], d_r.at[at], sibling)
        return remote(gacc.at[t, (1 - c) * 2 + j], drecv.at[at], d_s.at[at], d_r.at[at], sibling)

    def copy_x(t, j):
        at = (t, j)
        return remote(gsend.at[at], grecv.at[at], x_s.at[at], x_r.at[at], facing)

    def copy_h(t, j):
        ref = half.at[t, c * 2 + j]
        return remote(ref, ref, h_s.at[t, j], h_r.at[t, j], sibling)

    def copy_q(j):
        return remote(sqs.at[j], sqr.at[j], q_s.at[j], q_r.at[j], facing)

    def copy_c(j):
        ref = coefs.at[c * 2 + j]
        return remote(ref, ref, c_s.at[j], c_r.at[j], sibling)

    def copy_n():
        return remote(nrm.at[c], nrm.at[c], n_s, n_r, sibling)

    def copy_m(t, off):
        ref = mx.at[t, me]
        return remote(ref, ref, m_s.at[t, off], m_r.at[t, off], peer(off))

    def copy_ef(off):
        to = {"feat": lax.rem(f + off, F)}
        return remote(exf.at[f], exf.at[f], ef_s.at[off], ef_r.at[off], to)

    def copy_es(off):
        to = {"samp": lax.rem(s + off, S)}
        return remote(exs.at[s], exs.at[s], es_s.at[off], es_r.at[off], to)

    def each(first, count, body):
        def step(at, carry):
            body(at)
            return carry

        lax.fori_loop(first, count, step, 0)

    barrier = pltpu.get_barrier_semaphore()
    for off in range(1, F * CORES):
        pl.semaphore_signal(barrier, inc=1, device_id=peer(off), device_id_type=MESH)
    for core in range(CORES):
        to = {"samp": (1 - x) * CORES + core}
        pl.semaphore_signal(barrier, inc=1, device_id=to, device_id_type=MESH)
    load_warm.start()
    each(0, G, lambda g: load(1 - y, g).start())
    each(0, G, lambda g: load(y, g).start())
    load_targets.start()

    def share(t, side, g):
        return jnp.dot(design[rows_at(side, g), :], half[t].reshape(C, K), preferred_element_type=F32)

    def products(acc, rows, chunk, order):
        turned[...] = chunk.T
        for p in order:
            cols = pl.ds(pl.multiple_of(p * W, W), W)
            piece = jnp.dot(turned[...], design[rows, cols], preferred_element_type=F32)
            acc[p, 0:K] = acc[p, 0:K] + piece

    def grad_group(t, side, g, order=tuple(range(pieces))):
        chunk = resid[t, side, pl.ds(g * PER, PER)].reshape(GROUP, K)
        products(gacc.at[t], rows_at(side, g), chunk, order)

    def corr_group(at):
        rows = pl.ds(pl.multiple_of(at * GROUP, GROUP), GROUP)
        products(cacc, rows, targets[rows, :], range(pieces))
        tall = 16

        def body(i, acc):
            block = design[pl.ds(pl.multiple_of(at * GROUP + i * tall, tall), tall), :].astype(F32)
            block = block * block
            return acc + block[:8] + block[8:]

        acc = lax.fori_loop(0, GROUP // tall, body, jnp.zeros((8, C), F32), unroll=4)
        for p in range(pieces):
            cacc[p, K : K + 8] = cacc[p, K : K + 8] + acc[:, p * W : (p + 1) * W]

    def send_group(t, g):
        if t == 0:
            load(1 - y, g).wait()
        part = share(t, 1 - y, g).astype(BF16).reshape(PER, b, K)
        for j in range(PER):
            ysend[t, g * PER + j] = part[j]
        if t == 0:
            @pl.when(g == 0)
            def _():
                pl.semaphore_wait(barrier, F * CORES + CORES - 1)
        for j in range(PER):
            copy_y(t, g * PER + j).start()

    def fold_group(t, g):
        mine[...] = share(t, y, g)
        for j in range(PER):
            k = g * PER + j
            own = mine[j * b : (j + 1) * b]
            copy_y(t, k).wait_recv()

            @pl.when(is_end)
            def _():
                zsend[t, k] = (own + yrecv[t, k].astype(F32)).astype(BF16)
                copy_fold(t, k).start()

            @pl.when(is_mid)
            def _():
                copy_fold(t, k).wait_recv()
                zsend[t, k] = (own + yrecv[t, k].astype(F32) + frecv[t, k].astype(F32)).astype(BF16)
                copy_middle(t, k).start()

    def resid_group(t, g):
        @pl.when(is_end)
        def _():
            for j in range(PER):
                copy_out(t, g * PER + j).wait_recv()
                copy_a(t, g * PER + j).start()

        @pl.when(is_mid)
        def _():
            rr = jnp.zeros((1, K), F32)
            ry = jnp.zeros((1, K), F32)
            for j in range(PER):
                k = g * PER + j
                at = pl.ds(pl.multiple_of(y * H + k * b, b), b)
                goal = targets[at, :].astype(F32)
                copy_middle(t, k).wait_recv()
                fitted = zsend[t, k].astype(F32) + erecv[t, k].astype(F32)
                rounded = (goal - fitted).astype(BF16)
                resid[t, y, k] = rounded
                copy_a(t, k).start()
                copy_out(t, k).start()
                wide = rounded.astype(F32)
                rr = rr + jnp.sum(wide * wide, axis=0, keepdims=True)
                ry = ry + jnp.sum(wide * goal, axis=0, keepdims=True)
            sums[t : t + 1] = sums[t : t + 1] + 0.5 * rr
            sums[T + t : T + t + 1] = sums[T + t : T + t + 1] + 0.5 * ry

        grad_group(t, y, g)

    def last_group(t, g):
        for j in range(PER):
            copy_a(t, g * PER + j).wait_recv()
        if isinstance(g, int):
            grad_group(t, 1 - y, g, ((1 - c) * 2, (1 - c) * 2 + 1))
            for j in range(2):
                copy_d(t, j).start()
            grad_group(t, 1 - y, g, (c * 2, c * 2 + 1))
        else:
            grad_group(t, 1 - y, g)

    lag_fold = 3 * mid
    lag_resid = G - 1 - mid
    lag_last = G + 1

    def run(t, first, count):
        def step(at):
            to_fold = at - lag_fold
            to_resid = at - lag_resid
            to_last = at - lag_last

            @pl.when((to_fold >= 0) & (to_fold < G))
            def _():
                fold_group(t, to_fold)

            @pl.when((to_resid >= 0) & (to_resid < G))
            def _():
                resid_group(t, to_resid)

            @pl.when(to_last >= 0)
            def _():
                last_group(t, to_last)

            if t == 0:
                @pl.when(at < G)
                def _():
                    corr_group(at * 2)
                    corr_group(at * 2 + 1)

        each(first, count, step)

    def chip_sum(t, j):
        p = c * 2 + j
        copy_d(t, j).wait_recv()
        if t == T:
            both = cacc[p] + dcrecv[j]
            sqs[j] = both[K : K + 8]
            copy_q(j).start()
            gsend[t, j] = both[:K].astype(BF16)
        else:
            gsend[t, j] = (gacc[t, p] + drecv[t, j]).astype(BF16)
        copy_x(t, j).start()

    def whole_sum(t, j):
        copy_x(t, j).wait_recv()
        return gsend[t, j].astype(F32) + grecv[t, j].astype(F32)

    def spread(t, rows):
        most = fold(jnp.concatenate(rows, axis=1), jnp.maximum)
        mx[t, me] = jnp.broadcast_to(most, (8, LANES))
        for off in range(1, F * CORES):
            copy_m(t, off).start()

    def highest(t):
        for off in range(1, F * CORES):
            copy_m(t, off).wait_recv()
        tile = functools.reduce(jnp.maximum, [mx[t, at] for at in range(F * CORES)])
        return jnp.max(tile[0:1], axis=1, keepdims=True)

    def add_row(at, row):
        sums[at : at + 1] = sums[at : at + 1] + 0.5 * row

    load_warm.wait()
    half[0] = warm[...].astype(BF16).reshape(pieces, W, K)
    each(0, G, lambda g: send_group(0, g))
    sums[...] = jnp.zeros_like(sums)
    cacc[...] = jnp.zeros_like(cacc)
    gacc[...] = jnp.zeros_like(gacc)
    for j in range(2):
        cur[j] = warm[pl.ds(pl.multiple_of((c * 2 + j) * W, W), W), :].T
        add_row(2 * T, fold(column_norms(cur[j]), jnp.add))
    nrm[c] = jnp.zeros((8, 2 * W), F32)
    load_targets.wait()
    each(0, G, lambda g: load(y, g).wait())

    penalty = None
    step_sizes = None
    for t in range(T):
        if t > 0:
            each(0, G, lambda g: send_group(t, g))
        if t == 0:
            run(0, 0, G)
            for j in range(2):
                copy_d(T, j).start()
            run(0, G, G + 2)
            for j in range(2):
                chip_sum(T, j)
            run(0, G + 2, G + 5)
            spread(T, [column_norms(whole_sum(T, j)) for j in range(2)])
            run(0, G + 5, 2 * G)
        elif t == ITERS:
            run(t, 0, 2 * G - 2)
            exf[f] = sums[...]
            for off in range(1, F):
                copy_ef(off).start()
            run(t, 2 * G - 2, 2 * G)
        else:
            run(t, 0, 2 * G)
        last_group(t, G - 1)
        if t == 0:
            penalty = highest(T) / (8.0 + 4.0 * index[0].astype(F32))
            step_sizes = []
            for j in range(2):
                copy_q(j).wait_recv()
                squares = jnp.sum(sqs[j] + sqr[j], axis=0, keepdims=True)
                step_sizes.append(0.5 / (1.0 + squares))
        for j in range(2):
            chip_sum(t, j)
        if t == ITERS:
            for off in range(1, F):
                copy_ef(off).wait_recv()
            exs[s] = functools.reduce(jnp.add, [exf[at] for at in range(F)])
            for off in range(1, S):
                copy_es(off).start()
        norms = []
        for j in range(2):
            gradient = whole_sum(t, j)
            norms.append(column_norms(gradient))
            if t < ITERS:
                at = pl.ds(pl.multiple_of((c * 2 + j) * W, W), W)
                keep = mask[t : t + 1, at].astype(F32)
                moved = cur[j] + step_sizes[j] * gradient
                moved_norms = column_norms(moved)
                cutoff = step_sizes[j] * penalty
                factor = jnp.maximum(moved_norms - cutoff, 0.0) / jnp.maximum(moved_norms, cutoff)
                after = (keep * factor) * moved
                cur[j] = after
                upright = after.T
                half[t + 1, c * 2 + j] = upright.astype(BF16)
                copy_h(t + 1, j).start()
                if t + 1 == ITERS:
                    coefs[c * 2 + j] = upright
                    copy_c(j).start()
                add_row(3 * T + t, fold(1.0 - keep, jnp.add))
                add_row(2 * T + t + 1, fold(column_norms(after), jnp.add))
            nrm[c, t : t + 1, j * W : (j + 1) * W] = norms[j]
        spread(t, norms)
        if t < ITERS:
            for j in range(2):
                copy_h(t + 1, j).wait_recv()

    copy_n().start()
    for j in range(2):
        copy_c(j).wait_recv()
    coef_out[...] = coefs[...].reshape(C, K)
    for off in range(1, S):
        copy_es(off).wait_recv()
    merged = functools.reduce(jnp.add, [exs[at] for at in range(S)])
    added_up = jnp.sum(merged, axis=1, keepdims=True)
    copy_n().wait_recv()
    lines = []
    for t in range(T):
        rr, ry, bn = (added_up[at : at + 1] for at in (t, T + t, 2 * T + t))
        scale = jnp.maximum(penalty, highest(t))
        primal = 0.5 * rr + penalty * bn
        ratio = penalty / scale
        dual = ratio * ry - 0.5 * ratio * ratio * rr
        lines.append((primal - dual) / (primal + 1.0))
        for core in range(CORES):
            corr_out[t : t + 1, core * 2 * W : (core + 1) * 2 * W] = nrm[core, t : t + 1, :] / scale
    for t in range(ITERS):
        lines.append(added_up[3 * T + t : 3 * T + t + 1])
    for at, line in enumerate(lines):
        info_out[at : at + 1, :] = jnp.broadcast_to(line, (1, LANES))

    for t in range(T):

        def drain(k):
            copy_y(t, k).wait_send()
            copy_fold(t, k).wait_send()
            copy_a(t, k).wait_send()

            @pl.when(is_mid)
            def _():
                copy_out(t, k).wait_send()

        each(0, G * PER, drain)
    for j in range(2):
        for t in range(T + 1):
            copy_d(t, j).wait_send()
            copy_x(t, j).wait_send()
        for t in range(1, T):
            copy_h(t, j).wait_send()
        copy_q(j).wait_send()
        copy_c(j).wait_send()
    copy_n().wait_send()
    for t in range(T + 1):
        for off in range(1, F * CORES):
            copy_m(t, off).wait_send()
    for off in range(1, F):
        copy_ef(off).wait_send()
    for off in range(1, S):
        copy_es(off).wait_send()


def finish(coef, corr, info, coef_out, corr_out, gaps_out, pruned_out):
    coef_out[...] = coef[...]
    corr_out[...] = corr[...]
    for at in range(ITERS + 1):
        gaps_out[at] = info[at, 0]
    for at in range(ITERS):
        pruned_out[at] = info[ITERS + 1 + at, 0]


def fused(design, targets, warm_start, active_mask, penalty_index):
    F, S = lax.axis_size("feat"), lax.axis_size("samp")
    R, C = design.shape
    K = targets.shape[1]
    T = ITERS + 1
    N = R // 2 // GROUP * PER
    b = GROUP // PER
    pieces = CORES * 2
    W = C // pieces
    dma = pltpu.SemaphoreType.DMA
    vmem = pl.BlockSpec(memory_space=pltpu.VMEM)
    anywhere = pl.BlockSpec(memory_space=pl.ANY)
    smem = pl.BlockSpec(memory_space=pltpu.SMEM)
    chunks = pltpu.VMEM((T, N, b, K), BF16)
    coefficients, correlations, info = pl.pallas_call(
        kernel,
        out_shape=(
            jax.ShapeDtypeStruct((C, K), F32),
            jax.ShapeDtypeStruct((T, C), F32),
            jax.ShapeDtypeStruct((8, LANES), F32),
        ),
        in_specs=[anywhere] * 3 + [vmem, smem],
        out_specs=(vmem,) * 3,
        scratch_shapes=[
            pltpu.VMEM((R, C), BF16),
            pltpu.VMEM((R, K), BF16),
            pltpu.VMEM((C, K), F32),
            pltpu.VMEM((T, pieces, W, K), BF16),
            pltpu.VMEM((2, K, W), F32),
            chunks,
            chunks,
            chunks,
            chunks,
            chunks,
            pltpu.VMEM((T, 2, N, b, K), BF16),
            pltpu.VMEM((GROUP, K), F32),
            pltpu.VMEM((K, GROUP), BF16),
            pltpu.VMEM((T, pieces, K, W), F32),
            pltpu.VMEM((pieces, K + 8, W), F32),
            pltpu.VMEM((T, 2, K, W), F32),
            pltpu.VMEM((2, K + 8, W), F32),
            pltpu.VMEM((T + 1, 2, K, W), BF16),
            pltpu.VMEM((T + 1, 2, K, W), BF16),
            pltpu.VMEM((2, 8, W), F32),
            pltpu.VMEM((2, 8, W), F32),
            pltpu.VMEM((pieces, W, K), F32),
            pltpu.VMEM((CORES, 8, 2 * W), F32),
            pltpu.VMEM((T + 1, F * CORES, 8, LANES), F32),
            pltpu.VMEM((STATS, LANES), F32),
            pltpu.VMEM((F, STATS, LANES), F32),
            pltpu.VMEM((S, STATS, LANES), F32),
        ]
        + [dma((2, N // PER)), dma, dma]
        + [dma((T, N))] * 8
        + [dma((T + 1, 2))] * 4
        + [dma((T, 2))] * 2
        + [dma((2,))] * 4
        + [dma, dma]
        + [dma((T + 1, F * CORES))] * 2
        + [dma((F,))] * 2
        + [dma((S,))] * 2,
        compiler_params=pltpu.CompilerParams(
            collective_id=0, has_side_effects=True, vmem_limit_bytes=62 * 1024 * 1024
        ),
    )(design, targets, warm_start, active_mask, penalty_index)
    return pl.pallas_call(
        finish,
        out_shape=(
            jax.ShapeDtypeStruct((C, K), F32),
            jax.ShapeDtypeStruct((T, C), F32),
            jax.ShapeDtypeStruct((T,), F32),
            jax.ShapeDtypeStruct((ITERS,), F32),
        ),
        in_specs=[vmem, vmem, smem],
        out_specs=(vmem, vmem, smem, smem),
    )(coefficients, correlations, info)


def group_norms(matrix):
    return jnp.sqrt(jnp.sum(matrix * matrix, axis=1))


def transpose_product(design, right_side):
    return lax.dot_general(
        design, right_side, (((0,), (0,)), ((), ())), preferred_element_type=jnp.float32
    )


def plain(design, targets, warm_start, active_mask, penalty_index):
    row_count, col_count = design.shape
    feat_size = lax.axis_size("feat")
    feat_slot = lax.axis_index("feat")
    block_rows = row_count // feat_size
    samp_first = (lax.axis_index("samp") == 0).astype(jnp.float32)
    corr_local = transpose_product(design, targets)
    squares_local = jnp.sum(jnp.square(design.astype(jnp.float32)), axis=0)
    corr_y, column_squares = lax.psum((corr_local, squares_local), "samp")
    penalty_max = lax.pmax(jnp.max(group_norms(corr_y)), "feat")
    penalty = penalty_max / (8.0 + 4.0 * penalty_index[0].astype(jnp.float32))
    step_sizes = 0.5 / (1.0 + column_squares)
    current = warm_start
    correlations = []
    relative_gaps = []
    pruned_counts = []
    own_targets = lax.dynamic_slice_in_dim(targets, feat_slot * block_rows, block_rows, 0)
    for iteration in range(ITERS + 1):
        current_half = current.astype(jnp.bfloat16)
        fitted_part = jnp.dot(design, current_half, preferred_element_type=jnp.float32)
        fitted = lax.psum(fitted_part, "feat")
        residual_all = (targets.astype(jnp.float32) - fitted).astype(jnp.bfloat16)
        residual = lax.dynamic_slice_in_dim(residual_all, feat_slot * block_rows, block_rows, 0)
        grad_local = transpose_product(design, residual_all)
        resid_float = residual.astype(jnp.float32)
        rr_local = jnp.sum(resid_float * resid_float)
        ry_local = jnp.sum(resid_float * own_targets.astype(jnp.float32))
        bn_local = samp_first * jnp.sum(group_norms(current))
        if iteration < ITERS:
            keep = active_mask[iteration].astype(jnp.float32)
            pruned_local = samp_first * jnp.sum(1.0 - keep)
        else:
            pruned_local = jnp.zeros((), jnp.float32)
        gradient = lax.psum(grad_local, "samp")
        grad_norms = group_norms(gradient)
        local_max = jnp.max(grad_norms)
        grad_top = lax.pmax(local_max, "feat")
        rr_sum, ry_sum, bn_sum, pruned_sum = lax.psum(
            (rr_local, ry_local, bn_local, pruned_local), ("feat", "samp")
        )
        scale = jnp.maximum(penalty, grad_top)
        correlations.append(grad_norms / scale)
        primal = 0.5 * rr_sum + penalty * bn_sum
        ratio = penalty / scale
        dual = ratio * ry_sum - 0.5 * ratio * ratio * rr_sum
        relative_gaps.append((primal - dual) / (primal + 1.0))
        if iteration < ITERS:
            pruned_counts.append(pruned_sum)
            moved = current + step_sizes[:, None] * gradient
            moved_norms = group_norms(moved)
            cutoff = step_sizes * penalty
            factor = jnp.maximum(moved_norms - cutoff, 0.0) / jnp.maximum(moved_norms, cutoff)
            current = (keep * factor)[:, None] * moved
    return (current, jnp.stack(correlations), jnp.stack(relative_gaps), jnp.stack(pruned_counts))


def local(design, targets, warm_start, active_mask, penalty_index):
    feat, samp = lax.axis_size("feat"), lax.axis_size("samp")
    rows, cols = design.shape
    fits = (
        feat == 2 * LINE
        and samp == 2 * CORES
        and rows % (2 * GROUP) == 0
        and rows // (2 * GROUP) >= 6
        and cols % (2 * CORES * LANES) == 0
        and targets.shape[1] == LANES
    )
    form = fused if fits else plain
    return form(design, targets, warm_start, active_mask, penalty_index)


def solution(mesh):
    placed = (P("samp", "feat"), P("samp", None), P("feat", None), P(None, "feat"), P())
    return jax.shard_map(
        local,
        mesh=mesh,
        in_specs=placed,
        out_specs=(P("feat", None), P(None, "feat"), P(), P()),
        check_vma=False,
    )
```

time: 144 us -> 116 us (0.81)
  Pallas kernels: 142 us -> 115 us
    pallas_call x1, Pallas kernels: 140 us -> 113 us  [fused(): pl.pallas_call(kernel, out_shape=(jax.ShapeDtypeStruct((C, K), F32), jax....]
where the time goes in v1:
time: 116 us
  Pallas kernels  115 us (99%)
  between operations  1.29 us (1%)
    pallas_call x1, Pallas kernels, fused(): pl.pallas_call(kernel, out_shape=(jax.ShapeDtypeStruct((C, K), F32), jax....  113 us

profile of v1, /device:TPU:0, one launch (start us, length us, event | category | flops | bytes accessed | tf_op | source)
XLA Modules:
  0.0 116.2 jit_solution(8751999168184824233)
XLA Ops:
  1.3 113.0 %shard_map.84 = (f32[1024,128]{1,0:T(8,128)}, f32[3,1024]{1,0:T(4,128)}, f32[8,128]{1,0:T(8,128)}) custom-call(bf16[3584,1024]{1,0:T(8,128)(2,1)} %stored.1, bf16[3584,128]{1,0:T(8,128)(2,1)} %stored_targets.1, f32[1024,128]{1,0:T(8,128)} %stored_warm.1, s32[2,1024]{1,0:T(2,128)} %mask.1, s32[1]{0:T(128)S(6)} %copy.9.index), custom_call_target="tpu_custom_call" | custom-call | tf_op jit(solution)/shard_map/pallas_call | solution.py:472
  114.3 1.9 %shard_map.85 = (f32[1024,128]{1,0:T(8,128)}, f32[3,1024]{1,0:T(4,128)}, f32[3]{0:T(128)}, f32[2]{0:T(128)}) custom-call(f32[1024,128]{1,0:T(8,128)} %get-tuple-element.7.coef, f32[3,1024]{1,0:T(4,128)} %get-tuple-element.8.corr, f32[8,128]{1,0:T(8,128)} %get-tuple-element.9.info), custom_call_target="tpu_custom_call" | custom-call | tf_op jit(solution)/shard_map/pallas_call | solution.py:523

commit v2 on v1

--- a/solution.py
+++ b/solution.py
@@ -32,8 +32,8 @@
     stored, stored_targets, stored_warm, mask, index, coef_out, corr_out, info_out,
     design, targets, warm, half, cur, ysend, yrecv, zsend, frecv, erecv, resid, mine, turned,
     gacc, cacc, drecv, dcrecv, gsend, grecv, sqs, sqr, coefs, nrm, mx, sums, exf, exs,
-    l_s, t_s, w_s, y_s, y_r, z_s, f_r, e_r, b_s, a_s, a_r, d_s, d_r, x_s, x_r, h_s, h_r, q_s, q_r,
-    c_s, c_r, n_s, n_r, m_s, m_r, ef_s, ef_r, es_s, es_r,
+    l_s, o_s, t_s, w_s, y_s, z_s, b_s, a_s, d_s, dc_s, x_s, h_s, q_s, c_s, n_s, m_s, ef_s, es_s,
+    y_r, f_r, e_r, a_r, d_r, dc_r, h_r, x_r, m_r, q_r, c_r, n_r, ef_r, es_r,
 ):
     T = ITERS + 1
     F = exf.shape[0]
@@ -72,68 +72,74 @@
     def rows_at(side, g):
         return pl.ds(pl.multiple_of(side * H + g * GROUP, GROUP), GROUP)
 
-    def load(side, g):
-        at = rows_at(side, g)
-        return pltpu.make_async_copy(stored.at[at, :], design.at[at, :], l_s.at[side, g])
+    def load(g):
+        at = rows_at(1 - y, g)
+        return pltpu.make_async_copy(stored.at[at, :], design.at[at, :], l_s.at[g])
+
+    own_rows = pl.ds(pl.multiple_of(y * H, H), H)
+    load_own = pltpu.make_async_copy(stored.at[own_rows, :], design.at[own_rows, :], o_s)
 
     load_targets = pltpu.make_async_copy(stored_targets, targets, t_s)
     load_warm = pltpu.make_async_copy(stored_warm, warm, w_s)
 
     def copy_y(t, k):
         at = (t, k)
-        return remote(ysend.at[at], yrecv.at[at], y_s.at[at], y_r.at[at], across)
+        return remote(ysend.at[at], yrecv.at[at], y_s, y_r.at[k], across)
 
     def copy_fold(t, k):
         at = (t, k)
-        return remote(zsend.at[at], frecv.at[at], z_s.at[at], f_r.at[at], nearby)
+        return remote(zsend.at[at], frecv.at[at], z_s, f_r.at[k], nearby)
 
     def copy_middle(t, k):
         at = (t, k)
-        return remote(zsend.at[at], erecv.at[at], z_s.at[at], e_r.at[at], middle)
+        return remote(zsend.at[at], erecv.at[at], z_s, e_r.at[k], middle)
 
     def copy_out(t, k):
         ref = resid.at[t, y, k]
-        return remote(ref, ref, b_s.at[t, k], f_r.at[t, k], nearby)
+        return remote(ref, ref, b_s, f_r.at[k], nearby)
 
     def copy_a(t, k):
         ref = resid.at[t, y, k]
-        return remote(ref, ref, a_s.at[t, k], a_r.at[t, k], across)
+        return remote(ref, ref, a_s, a_r.at[k], across)
 
     def copy_d(t, j):
         at = (t, j)
         if t == T:
-            return remote(cacc.at[(1 - c) * 2 + j], dcrecv.at[j], d_s.at[at], d_r.at[at], sibling)
-        return remote(gacc.at[t, (1 - c) * 2 + j], drecv.at[at], d_s.at[at], d_r.at[at], sibling)
+            return remote(cacc.at[(1 - c) * 2 + j], dcrecv.at[j], dc_s, dc_r.at[j], sibling)
+        return remote(gacc.at[t, (1 - c) * 2 + j], drecv.at[at], d_s, d_r.at[j], sibling)
 
     def copy_x(t, j):
         at = (t, j)
-        return remote(gsend.at[at], grecv.at[at], x_s.at[at], x_r.at[at], facing)
+        return remote(gsend.at[at], grecv.at[at], x_s, x_r.at[at], facing)
 
     def copy_h(t, j):
         ref = half.at[t, c * 2 + j]
-        return remote(ref, ref, h_s.at[t, j], h_r.at[t, j], sibling)
-
-    def copy_q(j):
-        return remote(sqs.at[j], sqr.at[j], q_s.at[j], q_r.at[j], facing)
-
-    def copy_c(j):
-        ref = coefs.at[c * 2 + j]
-        return remote(ref, ref, c_s.at[j], c_r.at[j], sibling)
+        return remote(ref, ref, h_s, h_r.at[j], sibling)
+
+    def copy_q():
+        return remote(sqs, sqr, q_s, q_r, facing)
+
+    def copy_c():
+        ref = coefs.at[pl.ds(c * 2, 2)]
+        return remote(ref, ref, c_s, c_r, sibling)
 
     def copy_n():
         return remote(nrm.at[c], nrm.at[c], n_s, n_r, sibling)
 
     def copy_m(t, off):
         ref = mx.at[t, me]
-        return remote(ref, ref, m_s.at[t, off], m_r.at[t, off], peer(off))
+        return remote(ref, ref, m_s, m_r.at[t], peer(off))
 
     def copy_ef(off):
         to = {"feat": lax.rem(f + off, F)}
-        return remote(exf.at[f], exf.at[f], ef_s.at[off], ef_r.at[off], to)
+        return remote(exf.at[f], exf.at[f], ef_s, ef_r, to)
 
     def copy_es(off):
         to = {"samp": lax.rem(s + off, S)}
-        return remote(exs.at[s], exs.at[s], es_s.at[off], es_r.at[off], to)
+        return remote(exs.at[s], exs.at[s], es_s, es_r, to)
+
+    others_f = exf.at[pl.ds(0, F - 1)]
+    others_s = exs.at[pl.ds(0, S - 1)]
 
     def each(first, count, body):
         def step(at, carry):
@@ -149,8 +155,8 @@
         to = {"samp": (1 - x) * CORES + core}
         pl.semaphore_signal(barrier, inc=1, device_id=to, device_id_type=MESH)
     load_warm.start()
-    each(0, G, lambda g: load(1 - y, g).start())
-    each(0, G, lambda g: load(y, g).start())
+    each(0, G, lambda g: load(g).start())
+    load_own.start()
     load_targets.start()
 
     def share(t, side, g):
@@ -181,16 +187,14 @@
         for p in range(pieces):
             cacc[p, K : K + 8] = cacc[p, K : K + 8] + acc[:, p * W : (p + 1) * W]
 
-    def send_group(t, g):
+    def send_group(t, g, ready=True):
         if t == 0:
-            load(1 - y, g).wait()
+            load(g).wait()
         part = share(t, 1 - y, g).astype(BF16).reshape(PER, b, K)
         for j in range(PER):
             ysend[t, g * PER + j] = part[j]
-        if t == 0:
-            @pl.when(g == 0)
-            def _():
-                pl.semaphore_wait(barrier, F * CORES + CORES - 1)
+        if not ready:
+            pl.semaphore_wait(barrier, F * CORES + CORES - 1)
         for j in range(PER):
             copy_y(t, g * PER + j).start()
 
@@ -288,7 +292,6 @@
         if t == T:
             both = cacc[p] + dcrecv[j]
             sqs[j] = both[K : K + 8]
-            copy_q(j).start()
             gsend[t, j] = both[:K].astype(BF16)
         else:
             gsend[t, j] = (gacc[t, p] + drecv[t, j]).astype(BF16)
@@ -305,8 +308,8 @@
             copy_m(t, off).start()
 
     def highest(t):
-        for off in range(1, F * CORES):
-            copy_m(t, off).wait_recv()
+        several = mx.at[t, pl.ds(0, F * CORES - 1)]
+        remote(several, several, m_s, m_r.at[t], peer(1)).wait_recv()
         tile = functools.reduce(jnp.maximum, [mx[t, at] for at in range(F * CORES)])
         return jnp.max(tile[0:1], axis=1, keepdims=True)
 
@@ -315,7 +318,8 @@
 
     load_warm.wait()
     half[0] = warm[...].astype(BF16).reshape(pieces, W, K)
-    each(0, G, lambda g: send_group(0, g))
+    send_group(0, 0, False)
+    each(1, G, lambda g: send_group(0, g))
     sums[...] = jnp.zeros_like(sums)
     cacc[...] = jnp.zeros_like(cacc)
     gacc[...] = jnp.zeros_like(gacc)
@@ -324,7 +328,7 @@
         add_row(2 * T, fold(column_norms(cur[j]), jnp.add))
     nrm[c] = jnp.zeros((8, 2 * W), F32)
     load_targets.wait()
-    each(0, G, lambda g: load(y, g).wait())
+    load_own.wait()
 
     penalty = None
     step_sizes = None
@@ -338,6 +342,7 @@
             run(0, G, G + 2)
             for j in range(2):
                 chip_sum(T, j)
+            copy_q().start()
             run(0, G + 2, G + 5)
             spread(T, [column_norms(whole_sum(T, j)) for j in range(2)])
             run(0, G + 5, 2 * G)
@@ -353,15 +358,14 @@
         if t == 0:
             penalty = highest(T) / (8.0 + 4.0 * index[0].astype(F32))
             step_sizes = []
+            copy_q().wait_recv()
             for j in range(2):
-                copy_q(j).wait_recv()
                 squares = jnp.sum(sqs[j] + sqr[j], axis=0, keepdims=True)
                 step_sizes.append(0.5 / (1.0 + squares))
         for j in range(2):
             chip_sum(t, j)
         if t == ITERS:
-            for off in range(1, F):
-                copy_ef(off).wait_recv()
+            remote(others_f, others_f, ef_s, ef_r, across).wait_recv()
             exs[s] = functools.reduce(jnp.add, [exf[at] for at in range(F)])
             for off in range(1, S):
                 copy_es(off).start()
@@ -383,21 +387,20 @@
                 copy_h(t + 1, j).start()
                 if t + 1 == ITERS:
                     coefs[c * 2 + j] = upright
-                    copy_c(j).start()
                 add_row(3 * T + t, fold(1.0 - keep, jnp.add))
                 add_row(2 * T + t + 1, fold(column_norms(after), jnp.add))
             nrm[c, t : t + 1, j * W : (j + 1) * W] = norms[j]
         spread(t, norms)
+        if t + 1 == ITERS:
+            copy_c().start()
         if t < ITERS:
             for j in range(2):
                 copy_h(t + 1, j).wait_recv()
 
     copy_n().start()
-    for j in range(2):
-        copy_c(j).wait_recv()
+    copy_c().wait_recv()
     coef_out[...] = coefs[...].reshape(C, K)
-    for off in range(1, S):
-        copy_es(off).wait_recv()
+    remote(others_s, others_s, es_s, es_r, sibling).wait_recv()
     merged = functools.reduce(jnp.add, [exs[at] for at in range(S)])
     added_up = jnp.sum(merged, axis=1, keepdims=True)
     copy_n().wait_recv()
@@ -416,34 +419,27 @@
     for at, line in enumerate(lines):
         info_out[at : at + 1, :] = jnp.broadcast_to(line, (1, LANES))
 
-    for t in range(T):
-
-        def drain(k):
-            copy_y(t, k).wait_send()
-            copy_fold(t, k).wait_send()
-            copy_a(t, k).wait_send()
-
-            @pl.when(is_mid)
-            def _():
-                copy_out(t, k).wait_send()
-
-        each(0, G * PER, drain)
-    for j in range(2):
-        for t in range(T + 1):
-            copy_d(t, j).wait_send()
-            copy_x(t, j).wait_send()
-        for t in range(1, T):
-            copy_h(t, j).wait_send()
-        copy_q(j).wait_send()
-        copy_c(j).wait_send()
-    copy_n().wait_send()
-    for t in range(T + 1):
-        for off in range(1, F * CORES):
-            copy_m(t, off).wait_send()
-    for off in range(1, F):
-        copy_ef(off).wait_send()
-    for off in range(1, S):
-        copy_es(off).wait_send()
+    def drain(ref, sem):
+        remote(ref, ref, sem, n_r, sibling).wait_send()
+
+    drain(ysend, y_s)
+    drain(zsend, z_s)
+    drain(ysend, a_s)
+
+    @pl.when(is_mid)
+    def _():
+        drain(ysend, b_s)
+
+    drain(gacc.at[:, pl.ds(0, 2)], d_s)
+    drain(cacc.at[pl.ds(0, 2)], dc_s)
+    drain(gsend, x_s)
+    drain(half.at[pl.ds(0, ITERS), pl.ds(0, 2)], h_s)
+    drain(sqs, q_s)
+    drain(coefs.at[pl.ds(0, 2)], c_s)
+    drain(nrm.at[0], n_s)
+    drain(mx.at[:, pl.ds(0, F * CORES - 1)], m_s)
+    drain(others_f, ef_s)
+    drain(others_s, es_s)
 
 
 def finish(coef, corr, info, coef_out, corr_out, gaps_out, pruned_out):
@@ -507,15 +503,12 @@
             pltpu.VMEM((F, STATS, LANES), F32),
             pltpu.VMEM((S, STATS, LANES), F32),
         ]
-        + [dma((2, N // PER)), dma, dma]
-        + [dma((T, N))] * 8
-        + [dma((T + 1, 2))] * 4
-        + [dma((T, 2))] * 2
-        + [dma((2,))] * 4
-        + [dma, dma]
-        + [dma((T + 1, F * CORES))] * 2
-        + [dma((F,))] * 2
-        + [dma((S,))] * 2,
+        + [dma((N // PER,))]
+        + [dma] * 17
+        + [dma((N,))] * 4
+        + [dma((2,))] * 3
+        + [dma((T + 1, 2)), dma((T + 1,))]
+        + [dma] * 5,
         compiler_params=pltpu.CompilerParams(
             collective_id=0, has_side_effects=True, vmem_limit_bytes=62 * 1024 * 1024
         ),

time: 116 us -> 112 us (0.966)
  Pallas kernels: 115 us -> 110 us
    pallas_call x1, Pallas kernels: 113 us -> 108 us  [fused(): pl.pallas_call(kernel, out_shape=(jax.ShapeDtypeStruct((C, K), F32), jax....]
where the time goes in v2:
time: 112 us; the launch traced here: 111 us
  Pallas kernels  110 us (98%)
  between operations  1.29 us (1%)
    pallas_call x1, Pallas kernels, fused(): pl.pallas_call(kernel, out_shape=(jax.ShapeDtypeStruct((C, K), F32), jax....  108 us

profile of v2, /device:TPU:0, one launch (start us, length us, event | category | flops | bytes accessed | tf_op | source)
XLA Modules:
  0.0 111.4 jit_solution(5600190798286753363)
XLA Ops:
  1.3 108.3 %shard_map.84 = (f32[1024,128]{1,0:T(8,128)}, f32[3,1024]{1,0:T(4,128)}, f32[8,128]{1,0:T(8,128)}) custom-call(bf16[3584,1024]{1,0:T(8,128)(2,1)} %stored.1, bf16[3584,128]{1,0:T(8,128)(2,1)} %stored_targets.1, f32[1024,128]{1,0:T(8,128)} %stored_warm.1, s32[2,1024]{1,0:T(2,128)} %mask.1, s32[1]{0:T(128)S(6)} %copy.9.index), custom_call_target="tpu_custom_call" | custom-call | tf_op jit(solution)/shard_map/pallas_call | solution.py:468
  109.5 1.9 %shard_map.85 = (f32[1024,128]{1,0:T(8,128)}, f32[3,1024]{1,0:T(4,128)}, f32[3]{0:T(128)}, f32[2]{0:T(128)}) custom-call(f32[1024,128]{1,0:T(8,128)} %get-tuple-element.7.coef, f32[3,1024]{1,0:T(4,128)} %get-tuple-element.8.corr, f32[8,128]{1,0:T(8,128)} %get-tuple-element.9.info), custom_call_target="tpu_custom_call" | custom-call | tf_op jit(solution)/shard_map/pallas_call | solution.py:516

commit v3 on v2

--- a/solution.py
+++ b/solution.py
@@ -12,7 +12,8 @@
 BF16 = jnp.bfloat16
 LANES = 128
 GROUP = 256
-PER = 2
+PER = 4
+SHIFT = 1
 LINE = 4
 CORES = 2
 STATS = 16
@@ -29,19 +30,20 @@
 
 
 def kernel(
-    stored, stored_targets, stored_warm, mask, index, coef_out, corr_out, info_out,
-    design, targets, warm, half, cur, ysend, yrecv, zsend, frecv, erecv, resid, mine, turned,
+    stored, stored_targets, stored_warm, stored_mask, stored_index, coef_out, corr_out, info_out,
+    design, targets, warm, mask, index, half, cur, ysend, yrecv, zsend, frecv, erecv, resid, mine, turned,
     gacc, cacc, drecv, dcrecv, gsend, grecv, sqs, sqr, coefs, nrm, mx, sums, exf, exs,
-    l_s, o_s, t_s, w_s, y_s, z_s, b_s, a_s, d_s, dc_s, x_s, h_s, q_s, c_s, n_s, m_s, ef_s, es_s,
+    l_s, t_s, gv_r, tv_r, gv_s, tv_s, w_s, k_s, i_s, o_s, y_s, z_s, b_s, a_s, d_s, dc_s, x_s, h_s, q_s, c_s, n_s, m_s, ef_s, es_s,
     y_r, f_r, e_r, a_r, d_r, dc_r, h_r, x_r, m_r, q_r, c_r, n_r, ef_r, es_r,
 ):
     T = ITERS + 1
     F = exf.shape[0]
     S = exs.shape[0]
-    R, C = design.shape
+    R, C = stored.shape
     K = targets.shape[1]
     H = R // 2
     G = H // GROUP
+    full = G + SHIFT
     b = GROUP // PER
     pieces = CORES * 2
     W = C // pieces
@@ -52,6 +54,10 @@
     mid = lax.rem((z + 1) // 2, 2)
     is_mid = mid == 1
     is_end = mid == 0
+    takes = c == CORES - 1
+    gives = c == 0
+    held = G - SHIFT + SHIFT * c
+    count = held + SHIFT * c
     me = f * CORES + c
     near = z + 1 - 2 * lax.rem(z, 2)
     across = {"feat": z * 2 + 1 - y}
@@ -70,17 +76,31 @@
         return {"feat": to // CORES, "samp": x * CORES + lax.rem(to, CORES)}
 
     def rows_at(side, g):
+        return pl.ds(pl.multiple_of((side * full + g) * GROUP, GROUP), GROUP)
+
+    def stored_at(side, g):
         return pl.ds(pl.multiple_of(side * H + g * GROUP, GROUP), GROUP)
 
-    def load(g):
-        at = rows_at(1 - y, g)
-        return pltpu.make_async_copy(stored.at[at, :], design.at[at, :], l_s.at[g])
-
-    own_rows = pl.ds(pl.multiple_of(y * H, H), H)
-    load_own = pltpu.make_async_copy(stored.at[own_rows, :], design.at[own_rows, :], o_s)
-
-    load_targets = pltpu.make_async_copy(stored_targets, targets, t_s)
+    def load(side, g):
+        src, dst = stored.at[stored_at(side, g), :], design.at[rows_at(side, g), :]
+        return pltpu.make_async_copy(src, dst, l_s.at[side, g])
+
+    def give(side):
+        src, dst = stored.at[stored_at(side, G - 1), :], design.at[rows_at(side, full - 1), :]
+        return remote(src, dst, gv_s, gv_r.at[side], sibling)
+
+    def load_targets(side):
+        src, dst = stored_targets.at[side * H : (side + 1) * H, :], targets.at[side * full * GROUP : side * full * GROUP + H, :]
+        return pltpu.make_async_copy(src, dst, t_s.at[side])
+
+    def give_targets(side):
+        src = stored_targets.at[stored_at(side, G - 1), :]
+        return remote(src, targets.at[rows_at(side, full - 1), :], tv_s, tv_r.at[side], sibling)
+
     load_warm = pltpu.make_async_copy(stored_warm, warm, w_s)
+    load_mask = pltpu.make_async_copy(stored_mask, mask, k_s)
+    load_index = pltpu.make_async_copy(stored_index, index, i_s)
+    store_coefs = pltpu.make_async_copy(coefs, coef_out, o_s)
 
     def copy_y(t, k):
         at = (t, k)
@@ -148,16 +168,19 @@
 
         lax.fori_loop(first, count, step, 0)
 
+    load_warm.start()
+    each(0, held, lambda g: load(1 - y, g).start())
     barrier = pltpu.get_barrier_semaphore()
     for off in range(1, F * CORES):
         pl.semaphore_signal(barrier, inc=1, device_id=peer(off), device_id_type=MESH)
     for core in range(CORES):
         to = {"samp": (1 - x) * CORES + core}
         pl.semaphore_signal(barrier, inc=1, device_id=to, device_id_type=MESH)
-    load_warm.start()
-    each(0, G, lambda g: load(g).start())
-    load_own.start()
-    load_targets.start()
+    each(0, held, lambda g: load(y, g).start())
+    for side in range(2):
+        load_targets(side).start()
+    load_mask.start()
+    load_index.start()
 
     def share(t, side, g):
         return jnp.dot(design[rows_at(side, g), :], half[t].reshape(C, K), preferred_element_type=F32)
@@ -173,13 +196,13 @@
         chunk = resid[t, side, pl.ds(g * PER, PER)].reshape(GROUP, K)
         products(gacc.at[t], rows_at(side, g), chunk, order)
 
-    def corr_group(at):
-        rows = pl.ds(pl.multiple_of(at * GROUP, GROUP), GROUP)
+    def corr_group(side, g):
+        rows = rows_at(side, g)
         products(cacc, rows, targets[rows, :], range(pieces))
         tall = 16
 
         def body(i, acc):
-            block = design[pl.ds(pl.multiple_of(at * GROUP + i * tall, tall), tall), :].astype(F32)
+            block = design[pl.ds(pl.multiple_of((side * full + g) * GROUP + i * tall, tall), tall), :].astype(F32)
             block = block * block
             return acc + block[:8] + block[8:]
 
@@ -189,7 +212,14 @@
 
     def send_group(t, g, ready=True):
         if t == 0:
-            load(g).wait()
+            @pl.when(g < held)
+            def _():
+                load(1 - y, g).wait()
+
+            @pl.when(g >= held)
+            def _():
+                give(1 - y).wait_recv()
+
         part = share(t, 1 - y, g).astype(BF16).reshape(PER, b, K)
         for j in range(PER):
             ysend[t, g * PER + j] = part[j]
@@ -229,7 +259,7 @@
             ry = jnp.zeros((1, K), F32)
             for j in range(PER):
                 k = g * PER + j
-                at = pl.ds(pl.multiple_of(y * H + k * b, b), b)
+                at = pl.ds(pl.multiple_of(y * full * GROUP + k * b, b), b)
                 goal = targets[at, :].astype(F32)
                 copy_middle(t, k).wait_recv()
                 fitted = zsend[t, k].astype(F32) + erecv[t, k].astype(F32)
@@ -245,10 +275,10 @@
 
         grad_group(t, y, g)
 
-    def last_group(t, g):
+    def last_group(t, g, final=False):
         for j in range(PER):
             copy_a(t, g * PER + j).wait_recv()
-        if isinstance(g, int):
+        if final:
             grad_group(t, 1 - y, g, ((1 - c) * 2, (1 - c) * 2 + 1))
             for j in range(2):
                 copy_d(t, j).start()
@@ -257,20 +287,21 @@
             grad_group(t, 1 - y, g)
 
     lag_fold = 3 * mid
-    lag_resid = G - 1 - mid
-    lag_last = G + 1
-
-    def run(t, first, count):
+    lag_resid = jnp.where(is_mid, G - 2, count - 1)
+    lag_last = lag_resid + 2 + mid
+    steps = lag_last + count - 1
+
+    def run(t, first, until):
         def step(at):
             to_fold = at - lag_fold
             to_resid = at - lag_resid
             to_last = at - lag_last
 
-            @pl.when((to_fold >= 0) & (to_fold < G))
+            @pl.when((to_fold >= 0) & (to_fold < count))
             def _():
                 fold_group(t, to_fold)
 
-            @pl.when((to_resid >= 0) & (to_resid < G))
+            @pl.when((to_resid >= 0) & (to_resid < count))
             def _():
                 resid_group(t, to_resid)
 
@@ -279,12 +310,12 @@
                 last_group(t, to_last)
 
             if t == 0:
-                @pl.when(at < G)
+                @pl.when(at < count)
                 def _():
-                    corr_group(at * 2)
-                    corr_group(at * 2 + 1)
-
-        each(first, count, step)
+                    corr_group(0, at)
+                    corr_group(1, at)
+
+        each(first, until, step)
 
     def chip_sum(t, j):
         p = c * 2 + j
@@ -319,7 +350,15 @@
     load_warm.wait()
     half[0] = warm[...].astype(BF16).reshape(pieces, W, K)
     send_group(0, 0, False)
-    each(1, G, lambda g: send_group(0, g))
+
+    @pl.when(gives)
+    def _():
+        give(y).start()
+        give(1 - y).start()
+        for side in range(2):
+            give_targets(side).start()
+
+    each(1, count, lambda g: send_group(0, g))
     sums[...] = jnp.zeros_like(sums)
     cacc[...] = jnp.zeros_like(cacc)
     gacc[...] = jnp.zeros_like(gacc)
@@ -327,44 +366,56 @@
         cur[j] = warm[pl.ds(pl.multiple_of((c * 2 + j) * W, W), W), :].T
         add_row(2 * T, fold(column_norms(cur[j]), jnp.add))
     nrm[c] = jnp.zeros((8, 2 * W), F32)
-    load_targets.wait()
-    load_own.wait()
+    each(0, held, lambda g: load(y, g).wait())
+    for side in range(2):
+        load_targets(side).wait()
+
+    @pl.when(takes)
+    def _():
+        give(y).wait_recv()
+        for side in range(2):
+            give_targets(side).wait_recv()
+
 
     penalty = None
     step_sizes = None
     for t in range(T):
         if t > 0:
-            each(0, G, lambda g: send_group(t, g))
+            each(0, count, lambda g: send_group(t, g))
         if t == 0:
-            run(0, 0, G)
+            run(0, 0, count)
             for j in range(2):
                 copy_d(T, j).start()
-            run(0, G, G + 2)
+            run(0, count, count + 2)
             for j in range(2):
                 chip_sum(T, j)
             copy_q().start()
-            run(0, G + 2, G + 5)
+            run(0, count + 2, count + 5)
             spread(T, [column_norms(whole_sum(T, j)) for j in range(2)])
-            run(0, G + 5, 2 * G)
+            run(0, count + 5, steps)
         elif t == ITERS:
-            run(t, 0, 2 * G - 2)
+            run(t, 0, steps - 2)
             exf[f] = sums[...]
             for off in range(1, F):
                 copy_ef(off).start()
-            run(t, 2 * G - 2, 2 * G)
+            run(t, steps - 2, steps)
         else:
-            run(t, 0, 2 * G)
-        last_group(t, G - 1)
+            run(t, 0, steps)
+        last_group(t, count - 1, True)
+        for j in range(2):
+            chip_sum(t, j)
         if t == 0:
+            load_mask.wait()
+            load_index.wait()
             penalty = highest(T) / (8.0 + 4.0 * index[0].astype(F32))
             step_sizes = []
             copy_q().wait_recv()
             for j in range(2):
                 squares = jnp.sum(sqs[j] + sqr[j], axis=0, keepdims=True)
                 step_sizes.append(0.5 / (1.0 + squares))
-        for j in range(2):
-            chip_sum(t, j)
         if t == ITERS:
+            copy_c().wait_recv()
+            store_coefs.start()
             remote(others_f, others_f, ef_s, ef_r, across).wait_recv()
             exs[s] = functools.reduce(jnp.add, [exf[at] for at in range(F)])
             for off in range(1, S):
@@ -398,8 +449,6 @@
                 copy_h(t + 1, j).wait_recv()
 
     copy_n().start()
-    copy_c().wait_recv()
-    coef_out[...] = coefs[...].reshape(C, K)
     remote(others_s, others_s, es_s, es_r, sibling).wait_recv()
     merged = functools.reduce(jnp.add, [exs[at] for at in range(S)])
     added_up = jnp.sum(merged, axis=1, keepdims=True)
@@ -419,16 +468,29 @@
     for at, line in enumerate(lines):
         info_out[at : at + 1, :] = jnp.broadcast_to(line, (1, LANES))
 
+    store_coefs.wait()
+
     def drain(ref, sem):
         remote(ref, ref, sem, n_r, sibling).wait_send()
 
-    drain(ysend, y_s)
-    drain(zsend, z_s)
-    drain(ysend, a_s)
-
-    @pl.when(is_mid)
+    def drain_chunks(ref):
+        drain(ref, y_s)
+        drain(ref, z_s)
+        drain(ref, a_s)
+
+        @pl.when(is_mid)
+        def _():
+            drain(ref, b_s)
+
+    @pl.when(takes)
     def _():
-        drain(ysend, b_s)
+        drain_chunks(ysend)
+
+    @pl.when(gives)
+    def _():
+        drain_chunks(ysend.at[:, pl.ds(0, (G - SHIFT) * PER)])
+        drain(design.at[pl.ds(0, 2 * GROUP), :], gv_s)
+        drain(targets.at[pl.ds(0, 2 * GROUP), :], tv_s)
 
     drain(gacc.at[:, pl.ds(0, 2)], d_s)
     drain(cacc.at[pl.ds(0, 2)], dc_s)
@@ -443,7 +505,7 @@
 
 
 def finish(coef, corr, info, coef_out, corr_out, gaps_out, pruned_out):
-    coef_out[...] = coef[...]
+    coef_out[...] = coef[...].reshape(coef_out.shape)
     corr_out[...] = corr[...]
     for at in range(ITERS + 1):
         gaps_out[at] = info[at, 0]
@@ -456,7 +518,9 @@
     R, C = design.shape
     K = targets.shape[1]
     T = ITERS + 1
-    N = R // 2 // GROUP * PER
+    G = R // 2 // GROUP
+    full = G + SHIFT
+    N = full * PER
     b = GROUP // PER
     pieces = CORES * 2
     W = C // pieces
@@ -468,16 +532,18 @@
     coefficients, correlations, info = pl.pallas_call(
         kernel,
         out_shape=(
-            jax.ShapeDtypeStruct((C, K), F32),
+            jax.ShapeDtypeStruct((pieces, W, K), F32),
             jax.ShapeDtypeStruct((T, C), F32),
             jax.ShapeDtypeStruct((8, LANES), F32),
         ),
-        in_specs=[anywhere] * 3 + [vmem, smem],
-        out_specs=(vmem,) * 3,
+        in_specs=[anywhere] * 5,
+        out_specs=(anywhere, vmem, vmem),
         scratch_shapes=[
-            pltpu.VMEM((R, C), BF16),
-            pltpu.VMEM((R, K), BF16),
+            pltpu.VMEM((2 * full * GROUP, C), BF16),
+            pltpu.VMEM((2 * full * GROUP, K), BF16),
             pltpu.VMEM((C, K), F32),
+            pltpu.VMEM((ITERS, C), jnp.int32),
+            pltpu.SMEM((1,), jnp.int32),
             pltpu.VMEM((T, pieces, W, K), BF16),
             pltpu.VMEM((2, K, W), F32),
             chunks,
@@ -503,8 +569,9 @@
             pltpu.VMEM((F, STATS, LANES), F32),
             pltpu.VMEM((S, STATS, LANES), F32),
         ]
-        + [dma((N // PER,))]
-        + [dma] * 17
+        + [dma((2, G))]
+        + [dma((2,))] * 3
+        + [dma] * 20
         + [dma((N,))] * 4
         + [dma((2,))] * 3
         + [dma((T + 1, 2)), dma((T + 1,))]

time: 112 us -> 109 us (0.973)
  Pallas kernels: 110 us -> 108 us
    pallas_call x1, Pallas kernels: 108 us -> 106 us  [fused(): pl.pallas_call(kernel, out_shape=(jax.ShapeDtypeStruct((pieces, W, K), F3...]
where the time goes in v3:
time: 109 us
  Pallas kernels  108 us (99%)
  between operations  1.29 us (1%)
    pallas_call x1, Pallas kernels, fused(): pl.pallas_call(kernel, out_shape=(jax.ShapeDtypeStruct((pieces, W, K), F3...  106 us

profile of v3, /device:TPU:0, one launch (start us, length us, event | category | flops | bytes accessed | tf_op | source)
XLA Modules:
  0.0 109.2 jit_solution(11004669417434699081)
XLA Ops:
  1.3 106.0 %shard_map.84 = (f32[4,256,128]{2,1,0:T(8,128)}, f32[3,1024]{1,0:T(4,128)}, f32[8,128]{1,0:T(8,128)}) custom-call(bf16[3584,1024]{1,0:T(8,128)(2,1)} %stored.1, bf16[3584,128]{1,0:T(8,128)(2,1)} %stored_targets.1, f32[1024,128]{1,0:T(8,128)} %stored_warm.1, s32[2,1024]{1,0:T(2,128)} %stored_mask.1, s32[1]{0:T(128)S(6)} %copy.9.stored_index), custom_call_target="tpu_custom_call" | custom-call | tf_op jit(solution)/shard_map/pallas_call | solution.py:532
  107.3 1.9 %shard_map.85 = (f32[1024,128]{1,0:T(8,128)}, f32[3,1024]{1,0:T(4,128)}, f32[3]{0:T(128)}, f32[2]{0:T(128)}) custom-call(f32[4,256,128]{2,1,0:T(8,128)} %get-tuple-element.7.coef, f32[3,1024]{1,0:T(4,128)} %get-tuple-element.8.corr, f32[8,128]{1,0:T(8,128)} %get-tuple-element.9.info), custom_call_target="tpu_custom_call" | custom-call | tf_op jit(solution)/shard_map/pallas_call | solution.py:583

commit v4 on v3

--- a/solution.py
+++ b/solution.py
@@ -14,6 +14,12 @@
 GROUP = 256
 PER = 4
 SHIFT = 1
+MID_RESID = 9
+MID_LAST = 16
+END_RESID = 24
+LEAD = 3
+CORR_SUM = 3
+END_LAST = 13
 LINE = 4
 CORES = 2
 STATS = 16
@@ -120,7 +126,7 @@
 
     def copy_a(t, k):
         ref = resid.at[t, y, k]
-        return remote(ref, ref, a_s, a_r.at[k], across)
+        return remote(ref, ref, a_s, a_r.at[k // PER], across)
 
     def copy_d(t, j):
         at = (t, j)
@@ -228,56 +234,56 @@
         for j in range(PER):
             copy_y(t, g * PER + j).start()
 
-    def fold_group(t, g):
-        mine[...] = share(t, y, g)
-        for j in range(PER):
-            k = g * PER + j
-            own = mine[j * b : (j + 1) * b]
-            copy_y(t, k).wait_recv()
-
-            @pl.when(is_end)
-            def _():
-                zsend[t, k] = (own + yrecv[t, k].astype(F32)).astype(BF16)
-                copy_fold(t, k).start()
-
-            @pl.when(is_mid)
-            def _():
-                copy_fold(t, k).wait_recv()
-                zsend[t, k] = (own + yrecv[t, k].astype(F32) + frecv[t, k].astype(F32)).astype(BF16)
-                copy_middle(t, k).start()
-
-    def resid_group(t, g):
+    def fold_chunk(t, k):
+        g, j = k // PER, lax.rem(k, PER)
+
+        @pl.when(j == 0)
+        def _():
+            mine[...] = share(t, y, g)
+
+        own = mine[pl.ds(pl.multiple_of(j * b, b), b)]
+        copy_y(t, k).wait_recv()
+
         @pl.when(is_end)
         def _():
-            for j in range(PER):
-                copy_out(t, g * PER + j).wait_recv()
-                copy_a(t, g * PER + j).start()
+            zsend[t, k] = (own + yrecv[t, k].astype(F32)).astype(BF16)
+            copy_fold(t, k).start()
 
         @pl.when(is_mid)
         def _():
-            rr = jnp.zeros((1, K), F32)
-            ry = jnp.zeros((1, K), F32)
-            for j in range(PER):
-                k = g * PER + j
-                at = pl.ds(pl.multiple_of(y * full * GROUP + k * b, b), b)
-                goal = targets[at, :].astype(F32)
-                copy_middle(t, k).wait_recv()
-                fitted = zsend[t, k].astype(F32) + erecv[t, k].astype(F32)
-                rounded = (goal - fitted).astype(BF16)
-                resid[t, y, k] = rounded
-                copy_a(t, k).start()
-                copy_out(t, k).start()
-                wide = rounded.astype(F32)
-                rr = rr + jnp.sum(wide * wide, axis=0, keepdims=True)
-                ry = ry + jnp.sum(wide * goal, axis=0, keepdims=True)
+            copy_fold(t, k).wait_recv()
+            zsend[t, k] = (own + yrecv[t, k].astype(F32) + frecv[t, k].astype(F32)).astype(BF16)
+            copy_middle(t, k).start()
+
+    def resid_chunk(t, k):
+        @pl.when(is_end)
+        def _():
+            copy_out(t, k).wait_recv()
+            copy_a(t, k).start()
+
+        @pl.when(is_mid)
+        def _():
+            at = pl.ds(pl.multiple_of(y * full * GROUP + k * b, b), b)
+            goal = targets[at, :].astype(F32)
+            copy_middle(t, k).wait_recv()
+            fitted = zsend[t, k].astype(F32) + erecv[t, k].astype(F32)
+            rounded = (goal - fitted).astype(BF16)
+            resid[t, y, k] = rounded
+            copy_a(t, k).start()
+            copy_out(t, k).start()
+            wide = rounded.astype(F32)
+            rr = jnp.sum(wide * wide, axis=0, keepdims=True)
+            ry = jnp.sum(wide * goal, axis=0, keepdims=True)
             sums[t : t + 1] = sums[t : t + 1] + 0.5 * rr
             sums[T + t : T + t + 1] = sums[T + t : T + t + 1] + 0.5 * ry
 
-        grad_group(t, y, g)
+        @pl.when(lax.rem(k, PER) == PER - 1)
+        def _():
+            grad_group(t, y, k // PER)
 
     def last_group(t, g, final=False):
-        for j in range(PER):
-            copy_a(t, g * PER + j).wait_recv()
+        several = resid.at[t, 1 - y, pl.ds(g * PER, PER)]
+        remote(several, several, a_s, a_r.at[g], across).wait_recv()
         if final:
             grad_group(t, 1 - y, g, ((1 - c) * 2, (1 - c) * 2 + 1))
             for j in range(2):
@@ -286,34 +292,39 @@
         else:
             grad_group(t, 1 - y, g)
 
-    lag_fold = 3 * mid
-    lag_resid = jnp.where(is_mid, G - 2, count - 1)
-    lag_last = lag_resid + 2 + mid
-    steps = lag_last + count - 1
+    chunk_count = count * PER
+    lag_resid = jnp.where(is_mid, MID_RESID - 2 * c, END_RESID - 4 * c)
+    lag_last = lag_resid + jnp.where(is_mid, MID_LAST, END_LAST - 2 * c)
+
+    def lead(t):
+        return LEAD * PER * mid if t == 0 else 0
+
+    def steps(t):
+        return lead(t) + lag_last + chunk_count - PER
 
     def run(t, first, until):
         def step(at):
-            to_fold = at - lag_fold
-            to_resid = at - lag_resid
-            to_last = at - lag_last
-
-            @pl.when((to_fold >= 0) & (to_fold < count))
+            to_fold = at - lead(t)
+            to_resid = to_fold - lag_resid
+            to_last = to_fold - lag_last
+
+            @pl.when((to_fold >= 0) & (to_fold < chunk_count))
             def _():
-                fold_group(t, to_fold)
-
-            @pl.when((to_resid >= 0) & (to_resid < count))
+                fold_chunk(t, to_fold)
+
+            @pl.when((to_resid >= 0) & (to_resid < chunk_count))
             def _():
-                resid_group(t, to_resid)
-
-            @pl.when(to_last >= 0)
+                resid_chunk(t, to_resid)
+
+            @pl.when((to_last >= 0) & (lax.rem(to_last + PER, PER) == PER - 1))
             def _():
-                last_group(t, to_last)
+                last_group(t, to_last // PER)
 
             if t == 0:
-                @pl.when(at < count)
+                @pl.when((at < chunk_count) & (lax.rem(at, PER) == 0))
                 def _():
-                    corr_group(0, at)
-                    corr_group(1, at)
+                    corr_group(0, at // PER)
+                    corr_group(1, at // PER)
 
         each(first, until, step)
 
@@ -383,24 +394,25 @@
         if t > 0:
             each(0, count, lambda g: send_group(t, g))
         if t == 0:
-            run(0, 0, count)
+            second = lead(0) + chunk_count + CORR_SUM * PER
+            third = steps(0)
+            run(0, 0, chunk_count)
             for j in range(2):
                 copy_d(T, j).start()
-            run(0, count, count + 2)
+            run(0, chunk_count, second)
             for j in range(2):
                 chip_sum(T, j)
             copy_q().start()
-            run(0, count + 2, count + 5)
+            run(0, second, third)
             spread(T, [column_norms(whole_sum(T, j)) for j in range(2)])
-            run(0, count + 5, steps)
         elif t == ITERS:
-            run(t, 0, steps - 2)
+            run(t, 0, steps(t) - 2 * PER)
             exf[f] = sums[...]
             for off in range(1, F):
                 copy_ef(off).start()
-            run(t, steps - 2, steps)
+            run(t, steps(t) - 2 * PER, steps(t))
         else:
-            run(t, 0, steps)
+            run(t, 0, steps(t))
         last_group(t, count - 1, True)
         for j in range(2):
             chip_sum(t, j)
@@ -572,7 +584,8 @@
         + [dma((2, G))]
         + [dma((2,))] * 3
         + [dma] * 20
-        + [dma((N,))] * 4
+        + [dma((N,))] * 3
+        + [dma((full,))]
         + [dma((2,))] * 3
         + [dma((T + 1, 2)), dma((T + 1,))]
         + [dma] * 5,

time: 109 us -> 105 us (0.963)
  Pallas kernels: 108 us -> 103 us
    pallas_call x1, Pallas kernels: 106 us -> 101 us  [fused(): pl.pallas_call(kernel, out_shape=(jax.ShapeDtypeStruct((pieces, W, K), F3...]
where the time goes in v4:
time: 105 us
  Pallas kernels  103 us (98%)
  between operations  1.29 us (1%)
    pallas_call x1, Pallas kernels, fused(): pl.pallas_call(kernel, out_shape=(jax.ShapeDtypeStruct((pieces, W, K), F3...  101 us

profile of v4, /device:TPU:0, one launch (start us, length us, event | category | flops | bytes accessed | tf_op | source)
XLA Modules:
  0.0 104.5 jit_solution(13530841099956705622)
XLA Ops:
  1.3 101.3 %shard_map.84 = (f32[4,256,128]{2,1,0:T(8,128)}, f32[3,1024]{1,0:T(4,128)}, f32[8,128]{1,0:T(8,128)}) custom-call(bf16[3584,1024]{1,0:T(8,128)(2,1)} %stored.1, bf16[3584,128]{1,0:T(8,128)(2,1)} %stored_targets.1, f32[1024,128]{1,0:T(8,128)} %stored_warm.1, s32[2,1024]{1,0:T(2,128)} %stored_mask.1, s32[1]{0:T(128)S(6)} %copy.9.stored_index), custom_call_target="tpu_custom_call" | custom-call | tf_op jit(solution)/shard_map/pallas_call | solution.py:544
  102.6 1.9 %shard_map.85 = (f32[1024,128]{1,0:T(8,128)}, f32[3,1024]{1,0:T(4,128)}, f32[3]{0:T(128)}, f32[2]{0:T(128)}) custom-call(f32[4,256,128]{2,1,0:T(8,128)} %get-tuple-element.7.coef, f32[3,1024]{1,0:T(4,128)} %get-tuple-element.8.corr, f32[8,128]{1,0:T(8,128)} %get-tuple-element.9.info), custom_call_target="tpu_custom_call" | custom-call | tf_op jit(solution)/shard_map/pallas_call | solution.py:596

commit v5 on v4

--- a/solution.py
+++ b/solution.py
@@ -269,8 +269,8 @@
             fitted = zsend[t, k].astype(F32) + erecv[t, k].astype(F32)
             rounded = (goal - fitted).astype(BF16)
             resid[t, y, k] = rounded
+            copy_out(t, k).start()
             copy_a(t, k).start()
-            copy_out(t, k).start()
             wide = rounded.astype(F32)
             rr = jnp.sum(wide * wide, axis=0, keepdims=True)
             ry = jnp.sum(wide * goal, axis=0, keepdims=True)
@@ -465,6 +465,41 @@
     merged = functools.reduce(jnp.add, [exs[at] for at in range(S)])
     added_up = jnp.sum(merged, axis=1, keepdims=True)
     copy_n().wait_recv()
+    store_coefs.wait()
+
+    def drain(ref, sem):
+        remote(ref, ref, sem, n_r, sibling).wait_send()
+
+    def drain_chunks(ref):
+        drain(ref, y_s)
+        drain(ref, z_s)
+        drain(ref, a_s)
+
+        @pl.when(is_mid)
+        def _():
+            drain(ref, b_s)
+
+    @pl.when(takes)
+    def _():
+        drain_chunks(ysend)
+
+    @pl.when(gives)
+    def _():
+        drain_chunks(ysend.at[:, pl.ds(0, (G - SHIFT) * PER)])
+        drain(design.at[pl.ds(0, 2 * GROUP), :], gv_s)
+        drain(targets.at[pl.ds(0, 2 * GROUP), :], tv_s)
+
+    drain(gacc.at[:, pl.ds(0, 2)], d_s)
+    drain(cacc.at[pl.ds(0, 2)], dc_s)
+    drain(gsend, x_s)
+    drain(half.at[pl.ds(0, ITERS), pl.ds(0, 2)], h_s)
+    drain(sqs, q_s)
+    drain(coefs.at[pl.ds(0, 2)], c_s)
+    drain(nrm.at[0], n_s)
+    drain(mx.at[:, pl.ds(0, F * CORES - 1)], m_s)
+    drain(others_f, ef_s)
+    drain(others_s, es_s)
+
     lines = []
     for t in range(T):
         rr, ry, bn = (added_up[at : at + 1] for at in (t, T + t, 2 * T + t))
@@ -479,41 +514,6 @@
         lines.append(added_up[3 * T + t : 3 * T + t + 1])
     for at, line in enumerate(lines):
         info_out[at : at + 1, :] = jnp.broadcast_to(line, (1, LANES))
-
-    store_coefs.wait()
-
-    def drain(ref, sem):
-        remote(ref, ref, sem, n_r, sibling).wait_send()
-
-    def drain_chunks(ref):
-        drain(ref, y_s)
-        drain(ref, z_s)
-        drain(ref, a_s)
-
-        @pl.when(is_mid)
-        def _():
-            drain(ref, b_s)
-
-    @pl.when(takes)
-    def _():
-        drain_chunks(ysend)
-
-    @pl.when(gives)
-    def _():
-        drain_chunks(ysend.at[:, pl.ds(0, (G - SHIFT) * PER)])
-        drain(design.at[pl.ds(0, 2 * GROUP), :], gv_s)
-        drain(targets.at[pl.ds(0, 2 * GROUP), :], tv_s)
-
-    drain(gacc.at[:, pl.ds(0, 2)], d_s)
-    drain(cacc.at[pl.ds(0, 2)], dc_s)
-    drain(gsend, x_s)
-    drain(half.at[pl.ds(0, ITERS), pl.ds(0, 2)], h_s)
-    drain(sqs, q_s)
-    drain(coefs.at[pl.ds(0, 2)], c_s)
-    drain(nrm.at[0], n_s)
-    drain(mx.at[:, pl.ds(0, F * CORES - 1)], m_s)
-    drain(others_f, ef_s)
-    drain(others_s, es_s)
 
 
 def finish(coef, corr, info, coef_out, corr_out, gaps_out, pruned_out):

time: 105 us -> 105 us (level)
  no operation moved by 1% of the time
where the time goes in v5:
time: 105 us; the launch traced here: 104 us
  Pallas kernels  103 us (98%)
  between operations  1.29 us (1%)
    pallas_call x1, Pallas kernels, fused(): pl.pallas_call(kernel, out_shape=(jax.ShapeDtypeStruct((pieces, W, K), F3...  101 us

profile of v5, /device:TPU:0, one launch (start us, length us, event | category | flops | bytes accessed | tf_op | source)
XLA Modules:
  0.0 104.5 jit_solution(3807672779335226162)
XLA Ops:
  1.3 101.3 %shard_map.84 = (f32[4,256,128]{2,1,0:T(8,128)}, f32[3,1024]{1,0:T(4,128)}, f32[8,128]{1,0:T(8,128)}) custom-call(bf16[3584,1024]{1,0:T(8,128)(2,1)} %stored.1, bf16[3584,128]{1,0:T(8,128)(2,1)} %stored_targets.1, f32[1024,128]{1,0:T(8,128)} %stored_warm.1, s32[2,1024]{1,0:T(2,128)} %stored_mask.1, s32[1]{0:T(128)S(6)} %copy.9.stored_index), custom_call_target="tpu_custom_call" | custom-call | tf_op jit(solution)/shard_map/pallas_call | solution.py:544
  102.6 1.9 %shard_map.85 = (f32[1024,128]{1,0:T(8,128)}, f32[3,1024]{1,0:T(4,128)}, f32[3]{0:T(128)}, f32[2]{0:T(128)}) custom-call(f32[4,256,128]{2,1,0:T(8,128)} %get-tuple-element.7.coef, f32[3,1024]{1,0:T(4,128)} %get-tuple-element.8.corr, f32[8,128]{1,0:T(8,128)} %get-tuple-element.9.info), custom_call_target="tpu_custom_call" | custom-call | tf_op jit(solution)/shard_map/pallas_call | solution.py:596
